TPU v7x, 32 devices: a whole 2x2x4 slice. The times are simulated.
32 devices in a mesh: expert: 8 (over z, core), latent: 2 (over y), row: 2 (over x).
Axes of the slice: x: 2, y: 2, z: 4, core: 2. Of those that a mesh axis runs over, the one named last changes fastest.
Arguments:
- model_acts: bfloat16 [512, 8192], P('row', 'expert'), may hold values from -6 to 6
- enc_weight: bfloat16 [8192, 12288], P('expert', ('latent', 'row')), may hold values from -0.0625 to 0.0625
- dec_weight: bfloat16 [12288, 8192], P(('latent', 'row'), 'expert'), may hold values from -0.0546875 to 0.0546875
- enc_bias: float32 [12288], P('latent'), may hold values from -3 to 3
- dec_bias: float32 [8192], P('expert'), may hold values from -3 to 3
- enc_first: bfloat16 [8192, 12288], P('expert', ('latent', 'row')), may hold values from -0.119628906 to 0.119628906
- enc_second: bfloat16 [8192, 12288], P('expert', ('latent', 'row')), may hold values from 9.9658966e-05 to 0.0099487305
- dec_first: bfloat16 [12288, 8192], P(('latent', 'row'), 'expert'), may hold values from -0.119628906 to 0.119628906
- dec_second: bfloat16 [12288, 8192], P(('latent', 'row'), 'expert'), may hold values from 9.9658966e-05 to 0.0099487305
Outputs:
- encoder_next: bfloat16 [8192, 12288], P('expert', ('latent', 'row'))
- decoder_next: bfloat16 [12288, 8192], P(('latent', 'row'), 'expert')
- enc_first_next: bfloat16 [8192, 12288], P('expert', ('latent', 'row'))
- enc_second_next: bfloat16 [8192, 12288], P('expert', ('latent', 'row'))
- dec_first_next: bfloat16 [12288, 8192], P(('latent', 'row'), 'expert')
- dec_second_next: bfloat16 [12288, 8192], P(('latent', 'row'), 'expert')
- enc_bias_grad: float32 [12288], P(('latent', 'row'))
- dec_bias_grad: float32 [8192], P('expert')
All inputs are finite; a program needn't handle non-finite values.
Results may differ from a plain program's by a relative error of at most 0.005.
Values may be sent and summed in bfloat16 or wider, within the bound.
No kernel may reach another device: no remote copies, remote signals or barrier semaphores. Data moves between devices by JAX's collectives and lax.ppermute only.
A program may use at most 128 MiB of HBM per device.

v0:
```python
import jax
import jax.numpy as jnp
from jax import lax
from jax.sharding import PartitionSpec as P

EXPERTS = 8
D = 1024


beta_one = 0.9
beta_two = 0.999
learn_rate = 0.001
adam_eps = 1e-08
bias_one = 0.9999734386011124
bias_two = 0.09520785288629115
norm_eps = 1e-06
sparsity = 1.0


def adam_step(weight, moment_one, moment_two, gradient):
    first_next = beta_one * moment_one.astype(jnp.float32) + (1.0 - beta_one) * gradient
    second_next = beta_two * moment_two.astype(jnp.float32) + (1.0 - beta_two) * gradient * gradient
    stepped = weight.astype(jnp.float32) - learn_rate * (first_next / bias_one) / (
        jnp.sqrt(second_next / bias_two) + adam_eps
    )
    return (
        stepped.astype(jnp.bfloat16),
        first_next.astype(jnp.bfloat16),
        second_next.astype(jnp.bfloat16),
    )


def contract_rows(left, right):
    return lax.dot_general(
        left, right, (((0,), (0,)), ((), ())), preferred_element_type=jnp.float32
    )


def local(
    model_acts,
    enc_weight,
    dec_weight,
    enc_bias,
    dec_bias,
    enc_first,
    enc_second,
    dec_first,
    dec_second,
):
    shard_width = model_acts.shape[1]
    local_latents = enc_weight.shape[1]
    total_rows = model_acts.shape[0] * lax.axis_size("row")
    row_index = lax.axis_index("row")
    token_rows = lax.all_gather(model_acts, "row", axis=0, tiled=True)
    bias_here = lax.dynamic_slice_in_dim(enc_bias, row_index * local_latents, local_latents)
    column_pick = (jnp.arange(EXPERTS) == lax.axis_index("expert") * shard_width // D).astype(
        jnp.float32
    )
    decoder_wide = dec_weight.astype(jnp.float32)
    partial_sq = jnp.sum(decoder_wide * decoder_wide, axis=1)
    norm_sq = lax.psum(partial_sq[:, None] * column_pick[None, :], "expert")
    decoder_norms = jnp.sqrt(norm_sq + norm_eps)
    strength = jnp.sum(decoder_norms, axis=1)
    own_norm = jnp.sum(decoder_norms * column_pick[None, :], axis=1)
    preact_part = jnp.dot(token_rows, enc_weight, preferred_element_type=jnp.float32)
    preact = lax.psum_scatter(preact_part, "expert", scatter_dimension=0, tiled=True) + bias_here
    active = preact > 0
    latent_low = lax.all_gather(
        jnp.maximum(preact, 0.0).astype(jnp.bfloat16), "expert", axis=0, tiled=True
    )
    rebuilt_part = jnp.dot(latent_low, dec_weight, preferred_element_type=jnp.float32)
    rebuilt = lax.psum(rebuilt_part, ("latent", "row"))
    grad_rows = 2.0 * (rebuilt + dec_bias - token_rows.astype(jnp.float32)) / total_rows
    grad_low = grad_rows.astype(jnp.bfloat16)
    dec_main = contract_rows(latent_low, grad_low)
    col_total = jnp.sum(latent_low.astype(jnp.float32), axis=0)
    row_bias = jnp.sum(grad_rows, axis=0)
    back_part = lax.dot_general(
        grad_low, dec_weight, (((1,), (1,)), ((), ())), preferred_element_type=jnp.float32
    )
    penalty = sparsity * strength / total_rows
    back_grad = lax.psum_scatter(back_part, "expert", scatter_dimension=0, tiled=True) + penalty
    grad_pre = lax.all_gather(
        jnp.where(active, back_grad, 0.0).astype(jnp.bfloat16), "expert", axis=0, tiled=True
    )
    enc_main = contract_rows(token_rows, grad_pre)
    bias_sum = jnp.sum(grad_pre.astype(jnp.float32), axis=0)
    dec_grad = dec_main + sparsity * (col_total / total_rows)[:, None] * (
        dec_weight.astype(jnp.float32) / own_norm[:, None]
    )
    encoder_next, enc_first_next, enc_second_next = adam_step(
        enc_weight, enc_first, enc_second, enc_main
    )
    decoder_next, dec_first_next, dec_second_next = adam_step(
        dec_weight, dec_first, dec_second, dec_grad
    )
    return (
        encoder_next,
        decoder_next,
        enc_first_next,
        enc_second_next,
        dec_first_next,
        dec_second_next,
        bias_sum,
        row_bias,
    )


def solution(mesh):
    return jax.shard_map(
        local,
        mesh=mesh,
        in_specs=(
            P("row", "expert"),
            P("expert", ("latent", "row")),
            P(("latent", "row"), "expert"),
            P("latent"),
            P("expert"),
            P("expert", ("latent", "row")),
            P("expert", ("latent", "row")),
            P(("latent", "row"), "expert"),
            P(("latent", "row"), "expert"),
        ),
        out_specs=(
            P("expert", ("latent", "row")),
            P(("latent", "row"), "expert"),
            P("expert", ("latent", "row")),
            P("expert", ("latent", "row")),
            P(("latent", "row"), "expert"),
            P(("latent", "row"), "expert"),
            P(("latent", "row")),
            P("expert"),
        ),
        check_vma=False,
    )
```

profile of v0, /device:TPU:0, one launch (start us, length us, event | category | flops | bytes accessed | tf_op | source)
XLA Modules:
  0.0 464.4 jit_solution(15385568085803733185)
XLA Ops:
  7.2 0.0 all-gather.4.cloned.1.call-start
  7.2 0.7 all-gather.4.cloned.1.call-update
  7.9 0.0 reduce-scatter.3.cloned.1.call-start
  7.9 25.6 %all-gather.4.cloned.1.call-done = bf16[512,1024]{1,0:T(8,128)(2,1)} async-done(((bf16[256,1024]{1,0:T(8,128)(2,1)}), bf16[512,1024]{1,0:T(8,128)(2,1)}) %all-gather.4.cloned.1.call-update) | async-done | bytes 1048592 | tf_op jit(solution)/shard_map/all_gather | solution.py:54
  33.6 9.2 %fusion.14 = f32[512,3072]{1,0:T(8,128)} fusion(bf16[512,1024]{1,0:T(8,128)(2,1)} %all-gather.4.cloned.1.call-done, bf16[1024,3072]{1,0:T(8,128)(2,1)} %param.10), kind=kOutput, calls=%fused_computation.33 | convolution fusion | flops 3221225472 | bytes 13631488 | tf_op jit(solution)/shard_map/dot_general | solution.py:65
  42.8 0.0 copy-start.5
  42.8 0.0 reduce-scatter.3.cloned.1.call-update
  42.8 0.0 all-gather.6.cloned.1.call-start
  42.9 0.7 copy-done.5
  43.5 69.2 %reduce-scatter.3.cloned.1.call-done = f32[64,3072]{1,0:T(8,128)} async-done(((f32[512,3072]{1,0:T(8,128)}), f32[64,3072]{1,0:T(8,128)}) %reduce-scatter.3.cloned.1.call-update) | async-done | bytes 786448 | tf_op jit(solution)/shard_map/reduce_scatter | solution.py:66
  112.7 1.9 maximum_convert_fusion
  114.7 0.0 all-gather.6.cloned.1.call-update
  114.7 0.0 all-reduce.3.cloned.1.call-start
  114.7 36.9 %all-gather.6.cloned.1.call-done = bf16[512,3072]{1,0:T(8,128)(2,1)} async-done(((bf16[64,3072]{1,0:T(8,128)(2,1)}), bf16[512,3072]{1,0:T(8,128)(2,1)}) %all-gather.6.cloned.1.call-update) | async-done | bytes 3145744 | tf_op jit(solution)/shard_map/all_gather | solution.py:68
  151.7 8.5 %fusion.15 = f32[512,1024]{1,0:T(8,128)} fusion(bf16[512,3072]{1,0:T(8,128)(2,1)} %all-gather.6.cloned.1.call-done, bf16[3072,1024]{1,0:T(8,128)(2,1)} %param.11), kind=kOutput, calls=%fused_computation.34 | convolution fusion | flops 3221225472 | bytes 11534336 | tf_op jit(solution)/shard_map/dot_general | solution.py:71
  160.1 0.0 copy-start.3
  160.1 0.0 copy-start.6
  160.1 0.0 all-reduce.3.cloned.1.call-update
  160.2 0.0 all-reduce.5.cloned.1.call-start
  160.2 4.2 fusion
  164.4 0.7 broadcast_multiply_fusion
  165.1 0.0 all-reduce.5.cloned.1.call-update
  165.1 0.0 reduce-scatter.5.cloned.1.call-start
  165.2 63.5 %all-reduce.3.cloned.1.call-done = f32[512,1024]{1,0:T(8,128)} async-done(((f32[512,1024]{1,0:T(8,128)}), f32[512,1024]{1,0:T(8,128)}) %all-reduce.3.cloned.1.call-update) | async-done | bytes 2097168 | tf_op jit(solution)/shard_map/psum | solution.py:72
  228.7 0.0 copy-done.3
  228.7 0.0 copy-done.6
  228.7 2.6 fusion.11
  231.3 0.0 copy-start.4
  231.3 1.0 copy-done.4
  232.3 8.2 %fusion.16 = f32[512,3072]{1,0:T(8,128)} fusion(bf16[512,1024]{1,0:T(8,128)(2,1)S(1)} %get-tuple-element.33, bf16[3072,1024]{1,0:T(8,128)(2,1)} %param.11), kind=kOutput, calls=%fused_computation.35 | convolution fusion | flops 3221225472 | bytes 13631488 | tf_op jit(solution)/shard_map/dot_general | solution.py:78
  240.5 0.0 copy-start.2
  240.5 0.0 reduce-scatter.5.cloned.1.call-update
  240.6 0.0 all-gather.8.cloned.1.call-start
  240.6 43.2 %all-reduce.5.cloned.1.call-done = f32[3072,8]{0,1:T(8,128)} async-done(((f32[3072,8]{0,1:T(8,128)}), f32[3072,8]{0,1:T(8,128)}) %all-reduce.5.cloned.1.call-update) | async-done | bytes 98320 | tf_op jit(solution)/shard_map/psum | solution.py:61
  283.9 1.0 multiply_reduce_fusion
  284.9 73.1 %reduce-scatter.5.cloned.1.call-done = f32[64,3072]{1,0:T(8,128)} async-done(((f32[512,3072]{1,0:T(8,128)}), f32[64,3072]{1,0:T(8,128)}) %reduce-scatter.5.cloned.1.call-update) | async-done | bytes 786448 | tf_op jit(solution)/shard_map/reduce_scatter | solution.py:82
  357.9 0.0 copy-done.2
  357.9 2.0 select_convert_fusion
  359.9 0.0 all-gather.8.cloned.1.call-update
  360.0 8.9 %copy.23 = bf16[1024,3072]{0,1:T(8,128)(2,1)} copy(bf16[1024,3072]{1,0:T(8,128)(2,1)} %param.10) | data formatting | bytes 12582912 | tf_op args[1]
  368.9 8.6 %copy.24 = bf16[1024,3072]{0,1:T(8,128)(2,1)} copy(bf16[1024,3072]{1,0:T(8,128)(2,1)} %param.14) | data formatting | bytes 12582912 | tf_op args[5]
  377.5 0.0 copy-start
  377.5 8.8 %copy.25 = bf16[1024,3072]{0,1:T(8,128)(2,1)} copy(bf16[1024,3072]{1,0:T(8,128)(2,1)} %param.15) | data formatting | bytes 12582912 | tf_op args[6]
  386.3 0.0 copy-done
  386.3 0.6 convert_reduce_fusion.1
  387.0 21.2 %fusion.9 = (bf16[3072,1024]{1,0:T(8,128)(2,1)}, bf16[3072,1024]{1,0:T(8,128)(2,1)}, bf16[3072,1024]{1,0:T(8,128)(2,1)}) fusion(bf16[3072,1024]{1,0:T(8,128)(2,1)} %param.17, bf16[3072,1024]{1,0:T(8,128)(2,1)} %param.16, bf16[3072,1024]{1,0:T(8,128)(2,1)} %param.11, f32[3072]{0:T(1024)S(1)} %get-tuple-element.24, f32[3072]{0:T(1024)S(1)} %broadcast_multiply_fusion.1, ...), kind=kOutput, calls=%fused_computation.17 | convolution fusion | flops 3287285760 | bytes 41967616 | tf_op jit(solution)/shard_map/dot_general | solution.py:34
  408.2 0.0 all-gather.8.cloned.1.call-done
  408.2 22.1 %fusion.10 = (bf16[1024,3072]{0,1:T(8,128)(2,1)}, bf16[1024,3072]{0,1:T(8,128)(2,1)}, bf16[1024,3072]{0,1:T(8,128)(2,1)}) fusion(bf16[1024,3072]{0,1:T(8,128)(2,1)} %copy.25, bf16[1024,3072]{0,1:T(8,128)(2,1)} %copy.24, bf16[1024,3072]{0,1:T(8,128)(2,1)} %copy.23, bf16[512,3072]{1,0:T(8,128)(2,1)} %all-gather.8.cloned.1.call-done, ...), kind=kOutput, calls=%fused_computation.18 | convolution fusion | flops 3277848576 | bytes 41943040 | tf_op jit(solution)/shard_map/dot_general | solution.py:34
  430.3 8.6 %copy.28 = bf16[1024,3072]{1,0:T(8,128)(2,1)} copy(bf16[1024,3072]{0,1:T(8,128)(2,1)} %get-tuple-element.29) | data formatting | bytes 12582912
  438.9 8.6 %copy.26 = bf16[1024,3072]{1,0:T(8,128)(2,1)} copy(bf16[1024,3072]{0,1:T(8,128)(2,1)} %get-tuple-element.30) | data formatting | bytes 12582912
  447.6 0.0 copy-start.1
  447.6 8.8 %copy.27 = bf16[1024,3072]{1,0:T(8,128)(2,1)} copy(bf16[1024,3072]{0,1:T(8,128)(2,1)} %get-tuple-element.31) | data formatting | bytes 12582912
  456.3 0.0 copy-done.1
  456.3 1.2 convert_reduce_fusion
  (4 shorter events, 0.0 us)
Async XLA Ops:
  7.2 26.4 %all-gather.4.cloned.1.call-start = ((), (), s32[]{:S(2)}) async-start(), calls=%async_computation.2 | async-start | bytes 1572864 | tf_op jit(solution)/shard_map/all_gather | solution.py:54
  7.9 104.8 %reduce-scatter.3.cloned.1.call-start = ((), (), s32[]{:S(2)}) async-start(), calls=%async_computation.3 | async-start | bytes 7077888 | tf_op jit(solution)/shard_map/reduce_scatter | solution.py:66
  42.8 0.7 copy-start.5
  42.8 108.8 %all-gather.6.cloned.1.call-start = ((), (), s32[]{:S(2)}) async-start(), calls=%async_computation.4 | async-start | bytes 3538944 | tf_op jit(solution)/shard_map/all_gather | solution.py:68
  114.7 114.0 %all-reduce.3.cloned.1.call-start = ((), (), s32[]{:S(2)}) async-start(), calls=%async_computation.5 | async-start | bytes 4194304 | tf_op jit(solution)/shard_map/psum | solution.py:72
  160.1 68.6 %copy-start.3 = (bf16[512,1024]{1,0:T(8,128)(2,1)S(1)}, bf16[512,1024]{1,0:T(8,128)(2,1)}, u32[]{:S(2)}) copy-start(bf16[512,1024]{1,0:T(8,128)(2,1)} %all-gather.4.cloned.1.call-done) | copy-start | bytes 3145732
  160.1 68.6 %copy-start.6 = (f32[1024]{0:T(1024)S(1)}, f32[1024]{0:T(1024)}, u32[]{:S(2)}) copy-start(f32[1024]{0:T(1024)} %param.13) | copy-start | bytes 12292
  160.2 123.7 %all-reduce.5.cloned.1.call-start = ((), (), s32[]{:S(2)}) async-start(), calls=%async_computation.7 | async-start | bytes 196608 | tf_op jit(solution)/shard_map/psum | solution.py:61
  165.1 192.8 %reduce-scatter.5.cloned.1.call-start = ((), (), s32[]{:S(2)}) async-start(), calls=%async_computation.6 | async-start | bytes 7077888 | tf_op jit(solution)/shard_map/reduce_scatter | solution.py:82
  231.3 1.0 copy-start.4
  240.5 117.4 %copy-start.2 = (f32[64,3072]{1,0:T(8,128)S(1)}, f32[64,3072]{1,0:T(8,128)}, u32[]{:S(2)}) copy-start(f32[64,3072]{1,0:T(8,128)} %reduce-scatter.3.cloned.1.call-done) | copy-start | bytes 2359300
  240.6 167.6 %all-gather.8.cloned.1.call-start = ((), (), s32[]{:S(2)}) async-start(), calls=%async_computation.8 | async-start | bytes 3538944 | tf_op jit(solution)/shard_map/all_gather | solution.py:83
  377.5 8.8 %copy-start = (bf16[512,3072]{1,0:T(8,128)(2,1)S(1)}, bf16[512,3072]{1,0:T(8,128)(2,1)}, u32[]{:S(2)}) copy-start(bf16[512,3072]{1,0:T(8,128)(2,1)} %all-gather.6.cloned.1.call-done) | copy-start | bytes 9437188
  447.6 8.8 %copy-start.1 = (bf16[512,3072]{1,0:T(8,128)(2,1)S(1)}, bf16[512,3072]{1,0:T(8,128)(2,1)}, u32[]{:S(2)}) copy-start(bf16[512,3072]{1,0:T(8,128)(2,1)} %all-gather.8.cloned.1.call-done) | copy-start | bytes 9437188
Sparse Core Ops, SparseCore 0:
  9.5 23.9 all-gather.3
  42.9 69.7 reduce-scatter.2
  114.9 36.6 all-gather.5
  160.3 68.3 all-reduce.2
  231.4 52.3 all-reduce.4
  286.6 71.3 reduce-scatter.4
  360.1 36.6 all-gather.7
where the time goes:
time: 466 us; the launch traced here: 464 us
  waiting for transfers between devices  312 us (67%)
  matrix products  69.3 us (15%)
  local copies, waits for them, and re-layouts  54 us (12%)
  other arithmetic  14.3 us (3%)
  between operations  14.2 us (3%)
    reduce_scatter x1, waiting for transfers between devices, local(): lax.psum_scatter(back_part, 'expert', scatter_dimension=0, tiled=True)  73.1 us
    reduce_scatter x1, waiting for transfers between devices, local(): lax.psum_scatter(preact_part, 'expert', scatter_dimension=0, tiled=True)  69.2 us
    psum x1, waiting for transfers between devices, local(): rebuilt = lax.psum(rebuilt_part, ('latent', 'row'))  63.5 us
    unnamed x20, local copies, waits for them, and re-layouts  54 us
    dot_general x2, matrix products, contract_rows(): lax.dot_general(left, right, (((0,), (0,)), ((), ())), preferred_element_...  43.4 us
    psum x1, waiting for transfers between devices, local(): norm_sq = lax.psum(partial_sq[:, None] * column_pick[None, :], 'expert')  43.2 us
    all_gather x1, waiting for transfers between devices, local(): lax.all_gather(jnp.maximum(preact, 0.0).astype(jnp.bfloat16), 'expert', a...  36.9 us
    all_gather x1, waiting for transfers between devices, local(): token_rows = lax.all_gather(model_acts, 'row', axis=0, tiled=True)  25.6 us
  transfers between devices with their start and end apart: 7, of which 6 were waited for; matrix products, arithmetic and copies ran while one was open for 14% of the time, Pallas kernels for 0%

commit v1 on v0

v1 whole, which is shorter than its diff:
```python
import functools

import jax
import jax.numpy as jnp
from jax import lax
from jax.experimental import pallas as pl
from jax.experimental.pallas import tpu as pltpu
from jax.sharding import Mesh, PartitionSpec as P

D = 1024
GROUPS = 2
PIECES = 6
LANES = 128
VMEM_LIMIT = 24 * 2**20


beta_one = 0.9
beta_two = 0.999
learn_rate = 0.001
adam_eps = 1e-08
bias_one = 0.9999734386011124
bias_two = 0.09520785288629115
norm_eps = 1e-06
sparsity = 1.0

f32 = jnp.float32
bf16 = jnp.bfloat16


def adam_kernel(groups, decays, *refs):
    lefts, rights, refs = refs[:groups], refs[groups : 2 * groups], refs[2 * groups :]
    turned, refs = refs[-groups:], refs[:-groups]
    weight_ref, first_ref, second_ref = refs[:3]
    weight_out, first_out, second_out = refs[-3:]
    gradient = None
    for left, right, across in zip(lefts, rights, turned):
        across[...] = left[...].T
        part = jnp.dot(across[...], right[...], preferred_element_type=f32)
        gradient = part if gradient is None else gradient + part
    weight = weight_ref[...].astype(f32)
    if decays:
        scale = jnp.concatenate([refs[3][...]] * (weight.shape[1] // LANES), axis=1)
        gradient = gradient + scale * weight
    rate = bias_one / learn_rate
    tenth = (1.0 - beta_one) * gradient
    first_next = beta_one * first_ref[...].astype(f32) + tenth
    second_next = beta_two * second_ref[...].astype(f32) + (
        (1.0 - beta_two) / (1.0 - beta_one) ** 2 * (tenth * tenth)
    )
    square = second_next * (rate * rate / bias_two)
    stepped = weight - first_next / (square * lax.rsqrt(square) + rate * adam_eps)
    weight_out[...] = stepped.astype(bf16)
    first_out[...] = first_next.astype(bf16)
    second_out[...] = second_next.astype(bf16)


def adam_rows(lefts, rights, weight, first, second, tile, scale=None, done=None, begin=0, end=None):
    height, width = weight.shape
    end = height if end is None else end
    depth = lefts[0].shape[0]
    skip = begin // tile
    state = pl.BlockSpec((tile, width), lambda i: (i + skip, 0))
    in_specs = [pl.BlockSpec((depth, tile), lambda i: (0, i + skip))] * len(lefts)
    in_specs += [pl.BlockSpec((depth, width), lambda i: (0, 0))] * len(rights)
    in_specs += [state] * 3
    operands = [*lefts, *rights, weight, first, second]
    if scale is not None:
        in_specs.append(pl.BlockSpec((tile, LANES), lambda i: (i + skip, 0)))
        operands.append(scale)
    kernel = functools.partial(adam_kernel, len(lefts), scale is not None)
    aliases = {}
    if done is not None:
        fixed, inner = len(operands), kernel
        aliases = {fixed + i: i for i in range(3)}
        in_specs += [pl.BlockSpec(memory_space=pl.ANY)] * 3
        operands += done

        def kernel(*refs):
            inner(*refs[:fixed], *refs[fixed + 3 :])

    part = end - begin
    return pl.pallas_call(
        kernel,
        grid=(part // tile,),
        in_specs=in_specs,
        out_specs=[state] * 3,
        out_shape=[jax.ShapeDtypeStruct(weight.shape, bf16)] * 3,
        scratch_shapes=[pltpu.VMEM((tile, depth), bf16)] * len(lefts),
        input_output_aliases=aliases,
        cost_estimate=pl.CostEstimate(
            flops=2 * part * width * depth * len(lefts),
            bytes_accessed=12 * part * width,
            transcendentals=2 * part * width,
        ),
        compiler_params=pltpu.CompilerParams(vmem_limit_bytes=VMEM_LIMIT),
        name="adam",
    )(*operands)


def after(value, earlier):
    return value if earlier is None else lax.optimization_barrier((value, earlier))[0]


class Moves:
    def __init__(self, chips, latents, rows):
        self.chips, self.latents, self.rows = chips, latents, rows

    def sibling(self, value):
        return lax.ppermute(value, "core", [(0, 1), (1, 0)])

    def hop(self, value, first, last):
        top = self.chips - 1
        pairs = []
        for place in range(first, last + 1):
            pairs.append((place * 2, (place + 1) * 2))
            pairs.append(((top - place) * 2 + 1, (top - place - 1) * 2 + 1))
        return lax.ppermute(value, ("z", "core"), pairs)

    def flipped(self, blocks):
        return jnp.concatenate([blocks[:1], blocks[1:][::-1]], axis=0)

    def reduce_own(self, blocks, other, wire, earlier):
        other = self.flipped(other)
        carried = None
        for step in range(1, self.chips):
            part = blocks[step].astype(f32) + other[step].astype(f32)
            if carried is not None:
                part = part + carried.astype(f32)
            carried = self.hop(part.astype(wire), 0, step - 1)
        here = blocks[0].astype(f32) + other[0].astype(f32)
        away = after(self.sibling(carried), earlier)
        return here + (carried.astype(f32) + away.astype(f32))

    def gather_own(self, block):
        got, carried = [], block
        for step in range(1, self.chips):
            carried = self.hop(carried, step - 1, self.chips - 2)
            got.append(carried)
        got = jnp.stack(got)
        return jnp.concatenate([block[None], got + self.sibling(got)[::-1]], axis=0)

    def partner(self, value, step):
        axes = [("row", 1)]
        bit = 1
        while bit < self.latents:
            axes.append(("latent", bit))
            bit *= 2
        pairs = []
        for core, (axis, mask) in enumerate((axes[step], axes[len(axes) - 1 - step])):
            for latent in range(self.latents):
                for row in range(self.rows):
                    to = (latent ^ mask, row) if axis == "latent" else (latent, row ^ mask)
                    pairs.append(
                        (
                            (core * self.latents + latent) * self.rows + row,
                            (core * self.latents + to[0]) * self.rows + to[1],
                        )
                    )
        return lax.ppermute(value, ("core", "latent", "row"), pairs)

    def reduce_latents(self, part):
        steps = 1 + (self.latents.bit_length() - 1)
        total = part
        for step in range(steps):
            sent = total.astype(bf16)
            total = sent.astype(f32) + self.partner(sent, step).astype(f32)
        return total


def local(
    moves,
    model_acts,
    enc_weight,
    dec_weight,
    enc_bias,
    dec_bias,
    enc_first,
    enc_second,
    dec_first,
    dec_second,
):
    local_rows, shard_width = model_acts.shape
    local_latents = enc_weight.shape[1]
    chips = moves.chips
    total_rows = local_rows * moves.rows
    core, place, row_index = lax.axis_index("core"), lax.axis_index("z"), lax.axis_index("row")
    shards_per_expert = D // shard_width
    sub = local_rows // (GROUPS * chips)
    block_rows = sub * moves.rows

    bias_here = lax.dynamic_slice_in_dim(enc_bias, row_index * local_latents, local_latents)

    turned = model_acts.reshape(GROUPS, chips, sub, shard_width)
    step_of = jnp.where(core == 0, -jnp.arange(chips), jnp.arange(chips))
    turned = jnp.take(turned, (place + step_of) % chips, axis=1)

    tokens = []
    for group in range(GROUPS):
        own = turned[group]
        away = after(lax.ppermute(own, "row", [(0, 1), (1, 0)]), tokens[-1] if tokens else None)
        first, second = jnp.where(row_index == 0, own, away), jnp.where(row_index == 0, away, own)
        tokens.append(jnp.concatenate([first, second], axis=1).reshape(chips * block_rows, shard_width))

    wide = dec_weight.astype(f32)
    partial_sq = jnp.sum(wide * wide, axis=1)
    if shards_per_expert > 1:
        partial_sq = partial_sq + moves.sibling(partial_sq)
    own_norm = jnp.sqrt(partial_sq + norm_eps)
    penalty = sparsity * own_norm / (total_rows * shards_per_expert)

    lat, low, pre, col_total, row_bias, bias_sum = [], [], [], 0.0, 0.0, 0.0
    first_block = second_block = grad_low = None
    for group in range(GROUPS):
        part = jnp.dot(tokens[group], enc_weight, preferred_element_type=f32)
        part = part.reshape(chips, block_rows, local_latents)
        preact = moves.reduce_own(part, moves.sibling(part), f32, first_block) + bias_here
        active = preact > 0
        first_block = jnp.maximum(preact, 0.0).astype(bf16)
        latent = moves.gather_own(first_block)
        latent = latent.reshape(chips * block_rows, local_latents)
        rebuilt = jnp.dot(latent, dec_weight, preferred_element_type=f32)
        rebuilt = after(moves.reduce_latents(rebuilt), grad_low)
        grad_rows = 2.0 * (rebuilt + dec_bias - tokens[group].astype(f32)) / total_rows
        grad_low = grad_rows.astype(bf16)
        back = lax.dot_general(
            grad_low, dec_weight, (((1,), (1,)), ((), ())), preferred_element_type=f32
        )
        back = (back + penalty).astype(bf16).reshape(chips, block_rows, local_latents)
        back_grad = moves.reduce_own(back, moves.sibling(back), bf16, second_block)
        second_block = jnp.where(active, back_grad, 0.0).astype(bf16)
        grad_pre = moves.gather_own(second_block)
        grad_pre = grad_pre.reshape(chips * block_rows, local_latents)
        lat.append(latent)
        low.append(grad_low)
        pre.append(grad_pre)
        col_total = col_total + jnp.sum(latent.astype(f32), axis=0)
        row_bias = row_bias + jnp.sum(grad_rows, axis=0)
        bias_sum = bias_sum + jnp.sum(grad_pre.astype(f32), axis=0)

    scale = sparsity * col_total / (total_rows * own_norm)
    scale = jnp.broadcast_to(scale[:, None], (local_latents, LANES))
    piece_rows = local_latents // PIECES
    tile = 2 * LANES if piece_rows % (2 * LANES) == 0 else LANES
    done = None
    for piece in range(PIECES):
        begin = piece * piece_rows
        done = adam_rows(
            lat, low, dec_weight, dec_first, dec_second, tile, scale, done, begin, begin + piece_rows
        )
    decoder_next, dec_first_next, dec_second_next = done
    encoder_next, enc_first_next, enc_second_next = adam_rows(
        tokens, pre, enc_weight, enc_first, enc_second, LANES
    )
    return (
        encoder_next,
        decoder_next,
        enc_first_next,
        enc_second_next,
        dec_first_next,
        dec_second_next,
        bias_sum,
        row_bias,
    )


def solution(mesh):
    experts, latents, rows = (mesh.shape[name] for name in ("expert", "latent", "row"))
    fine = Mesh(
        mesh.devices.reshape(experts // 2, 2, latents, rows), ("z", "core", "latent", "row")
    )
    moves = Moves(experts // 2, latents, rows)
    expert = ("z", "core")
    enc, dec = P(expert, ("latent", "row")), P(("latent", "row"), expert)

    def body(*arrays):
        return local(moves, *arrays)

    return jax.shard_map(
        body,
        mesh=fine,
        in_specs=(P("row", expert), enc, dec, P("latent"), P(expert), enc, enc, dec, dec),
        out_specs=(enc, dec, enc, enc, dec, dec, P(("latent", "row")), P(expert)),
        check_vma=False,
    )
```

time: 466 us -> 290 us (0.62)
  waiting for transfers between devices: 312 us -> 85.4 us
  starting transfers between devices: 0.29 us -> 134 us
  matrix products: 69.3 us -> 13.8 us
  local copies, waits for them, and re-layouts: 54 us -> 6.04 us
  Pallas kernels: 0 us -> 33.2 us
  between operations: 14.2 us -> 1.44 us
    reduce_scatter x2 -> x0, waiting for transfers between devices: 142 us -> none  [the longest x1 73.1 us: local(): lax.psum_scatter(back_part, 'expert', scatter_dimension=0, tiled=True)]
    ppermute x0 -> x42, starting transfers between devices: none -> 134 us  [the longest x24 78.1 us: hop(): return lax.ppermute(value, ('z', 'core'), pairs)]
    psum x2 -> x0, waiting for transfers between devices: 107 us -> none  [the longest x1 63.5 us: local(): rebuilt = lax.psum(rebuilt_part, ('latent', 'row'))]
    ppermute x0 -> x42, waiting for transfers between devices: none -> 85.4 us  [the longest x24 50.3 us: hop(): return lax.ppermute(value, ('z', 'core'), pairs)]
    all_gather x3 -> x0, waiting for transfers between devices: 62.5 us -> none  [the longest x1 36.9 us: local(): lax.all_gather(jnp.maximum(preact, 0.0).astype(jnp.bfloat16), 'expert', a...]
    dot_general x4, matrix products: 61.1 us -> 10.1 us  [the longest x2 6.56 us: local(): part = jnp.dot(tokens[group], enc_weight, preferred_element_type=f32)]
    unnamed x20 -> x42, local copies, waits for them, and re-layouts: 54 us -> 4.96 us
    pallas_call x0 -> x7, Pallas kernels: none -> 33.2 us  [adam_rows(): pl.pallas_call(kernel, grid=(part // tile,), in_specs=in_specs, out_specs...]
  transfers between devices with their start and end apart: 7 -> 42, of which waited for: 6 -> 26; matrix products, arithmetic and copies ran while one was open for 14% -> 6% of each run, Pallas kernels for 0% -> 7%
where the time goes in v1:
time: 290 us; the launch traced here: 288 us
  starting transfers between devices  134 us (46%)
  waiting for transfers between devices  85.4 us (29%)
  Pallas kernels  33.2 us (11%)
  other arithmetic  13.8 us (5%)
  matrix products  13.8 us (5%)
  local copies, waits for them, and re-layouts  6.04 us (2%)
    ppermute x24, starting transfers between devices, hop(): return lax.ppermute(value, ('z', 'core'), pairs)  78.1 us
    ppermute x24, waiting for transfers between devices, hop(): return lax.ppermute(value, ('z', 'core'), pairs)  50.3 us
    ppermute x12, starting transfers between devices, sibling(): return lax.ppermute(value, 'core', [(0, 1), (1, 0)])  47.2 us
    pallas_call x7, Pallas kernels, adam_rows(): pl.pallas_call(kernel, grid=(part // tile,), in_specs=in_specs, out_specs...  33.2 us
    ppermute x4, waiting for transfers between devices, partner(): return lax.ppermute(value, ('core', 'latent', 'row'), pairs)  17 us
    ppermute x2, waiting for transfers between devices, local(): lax.ppermute(own, 'row', [(0, 1), (1, 0)])  11.8 us
    dot_general x2, matrix products, local(): part = jnp.dot(tokens[group], enc_weight, preferred_element_type=f32)  6.56 us
    ppermute x12, waiting for transfers between devices, sibling(): return lax.ppermute(value, 'core', [(0, 1), (1, 0)])  6.35 us
  transfers between devices with their start and end apart: 42, of which 26 were waited for; matrix products, arithmetic and copies ran while one was open for 6% of the time, Pallas kernels for 7%

profile of v1, /device:TPU:0, one launch (start us, length us, event | category | flops | bytes accessed | tf_op | source)
XLA Modules:
  0.0 287.6 jit_solution(196850741620238639)
XLA Ops:
  0.7 1.0 copy-done
  2.4 3.0 %collective-permute-start = (bf16[4,32,1024]{2,1,0:T(8,128)(2,1)S(1)}, bf16[4,32,1024]{2,1,0:T(8,128)(2,1)S(1)}, u32[]{:S(2)}, u32[]{:S(2)}) collective-permute-start(bf16[4,32,1024]{2,1,0:T(8,128)(2,1)S(1)} %get-tuple-element.70), channel_id=1, source_target_pairs={{0,1},{1,0},{2,3},{3,2},{4,5},{5,4},{6,7},{7,6},{8,9},{9,8},{10,11... | collective-permute-start | bytes 786440 | tf_op jit(solution)/shard_map/ppermute | solution.py:200
  5.5 7.1 %collective-permute-done = bf16[4,32,1024]{2,1,0:T(8,128)(2,1)S(1)} collective-permute-done((bf16[4,32,1024]{2,1,0:T(8,128)(2,1)S(1)}, bf16[4,32,1024]{2,1,0:T(8,128)(2,1)S(1)}, u32[]{:S(2)}, u32[]{:S(2)}) %collective-permute-start) | collective-permute-done | bytes 262176 | tf_op jit(solution)/shard_map/ppermute | solution.py:200
  12.7 4.7 %collective-permute-done.1 = bf16[4,32,1024]{2,1,0:T(8,128)(2,1)S(1)} collective-permute-done((bf16[4,32,1024]{2,1,0:T(8,128)(2,1)S(1)}, bf16[4,32,1024]{2,1,0:T(8,128)(2,1)S(1)}, u32[]{:S(2)}, u32[]{:S(2)}) %collective-permute-start.1) | collective-permute-done | bytes 262176 | tf_op jit(solution)/shard_map/ppermute | solution.py:200
  17.4 4.7 %fusion.46 = f32[256,3072]{1,0:T(8,128)S(1)} fusion(bf16[256,1024]{1,0:T(8,128)(2,1)S(1)} %bitcast.172, bf16[1024,3072]{1,0:T(8,128)(2,1)} %refs_4_.7), kind=kOutput, calls=%fused_computation.120 | convolution fusion | flops 1610612736 | bytes 9961472 | tf_op jit(solution)/shard_map/dot_general | solution.py:214
  22.3 1.8 fusion.47
  24.7 3.1 %collective-permute-done.2 = f32[4,64,3072]{2,1,0:T(8,128)S(1)} collective-permute-done((f32[4,64,3072]{2,1,0:T(8,128)S(1)}, f32[4,64,3072]{2,1,0:T(8,128)S(1)}, u32[]{:S(2)}, u32[]{:S(2)}) %collective-permute-start.2) | collective-permute-done | bytes 3145760 | tf_op jit(solution)/shard_map/ppermute | solution.py:109
  28.0 3.8 %collective-permute-start.3 = (f32[64,3072]{1,0:T(8,128)S(1)}, f32[64,3072]{1,0:T(8,128)S(1)}, u32[]{:S(2)}, u32[]{:S(2)}) collective-permute-start(f32[64,3072]{1,0:T(8,128)S(1)} %fusion.10), channel_id=1, source_target_pairs={{0,8},{28,20},{1,9},{29,21},{2,10},{30,22},{3,11},{31,23}} | collective-permute-start | bytes 2359304 | tf_op jit(solution)/shard_map/ppermute | solution.py:117
  32.5 3.8 %collective-permute-start.23 = (f32[64,3072]{1,0:T(8,128)S(1)}, f32[64,3072]{1,0:T(8,128)S(1)}, u32[]{:S(2)}, u32[]{:S(2)}) collective-permute-start(f32[64,3072]{1,0:T(8,128)S(1)} %fusion.2), channel_id=1, source_target_pairs={{0,8},{28,20},{1,9},{29,21},{2,10},{30,22},{3,11},{31,23}} | collective-permute-start | bytes 2359304 | tf_op jit(solution)/shard_map/ppermute | solution.py:117
  36.3 4.9 %collective-permute-done.3 = f32[64,3072]{1,0:T(8,128)S(1)} collective-permute-done((f32[64,3072]{1,0:T(8,128)S(1)}, f32[64,3072]{1,0:T(8,128)S(1)}, u32[]{:S(2)}, u32[]{:S(2)}) %collective-permute-start.3) | collective-permute-done | bytes 786464 | tf_op jit(solution)/shard_map/ppermute | solution.py:117
  41.3 4.4 %collective-permute-start.4 = (f32[64,3072]{1,0:T(8,128)S(1)}, f32[64,3072]{1,0:T(8,128)S(1)}, u32[]{:S(2)}, u32[]{:S(2)}) collective-permute-start(f32[64,3072]{1,0:T(8,128)S(1)} %fusion.12), channel_id=1, source_target_pairs={{0,8},{28,20},{8,16},{20,12},{1,9},{29,21},{9,17},{21,13},{2,10},{... | collective-permute-start | bytes 2359304 | tf_op jit(solution)/shard_map/ppermute | solution.py:117
  45.8 3.8 %collective-permute-done.23 = f32[64,3072]{1,0:T(8,128)S(1)} collective-permute-done((f32[64,3072]{1,0:T(8,128)S(1)}, f32[64,3072]{1,0:T(8,128)S(1)}, u32[]{:S(2)}, u32[]{:S(2)}) %collective-permute-start.23) | collective-permute-done | bytes 786464 | tf_op jit(solution)/shard_map/ppermute | solution.py:117
  49.8 4.4 %collective-permute-start.24 = (f32[64,3072]{1,0:T(8,128)S(1)}, f32[64,3072]{1,0:T(8,128)S(1)}, u32[]{:S(2)}, u32[]{:S(2)}) collective-permute-start(f32[64,3072]{1,0:T(8,128)S(1)} %fusion.4), channel_id=1, source_target_pairs={{0,8},{28,20},{8,16},{20,12},{1,9},{29,21},{9,17},{21,13},{2,10},{... | collective-permute-start | bytes 2359304 | tf_op jit(solution)/shard_map/ppermute | solution.py:117
  54.2 3.8 %collective-permute-done.4 = f32[64,3072]{1,0:T(8,128)S(1)} collective-permute-done((f32[64,3072]{1,0:T(8,128)S(1)}, f32[64,3072]{1,0:T(8,128)S(1)}, u32[]{:S(2)}, u32[]{:S(2)}) %collective-permute-start.4) | collective-permute-done | bytes 786464 | tf_op jit(solution)/shard_map/ppermute | solution.py:117
  58.2 4.4 %collective-permute-start.5 = (f32[64,3072]{1,0:T(8,128)S(1)}, f32[64,3072]{1,0:T(8,128)S(1)}, u32[]{:S(2)}, u32[]{:S(2)}) collective-permute-start(f32[64,3072]{1,0:T(8,128)S(1)} %fusion.14), channel_id=1, source_target_pairs={{0,8},{28,20},{8,16},{20,12},{16,24},{12,4},{1,9},{29,21},{9,17},{... | collective-permute-start | bytes 2359304 | tf_op jit(solution)/shard_map/ppermute | solution.py:117
  62.7 3.8 %collective-permute-done.24 = f32[64,3072]{1,0:T(8,128)S(1)} collective-permute-done((f32[64,3072]{1,0:T(8,128)S(1)}, f32[64,3072]{1,0:T(8,128)S(1)}, u32[]{:S(2)}, u32[]{:S(2)}) %collective-permute-start.24) | collective-permute-done | bytes 786464 | tf_op jit(solution)/shard_map/ppermute | solution.py:117
  66.6 4.4 %collective-permute-start.25 = (f32[64,3072]{1,0:T(8,128)S(1)}, f32[64,3072]{1,0:T(8,128)S(1)}, u32[]{:S(2)}, u32[]{:S(2)}) collective-permute-start(f32[64,3072]{1,0:T(8,128)S(1)} %fusion.6), channel_id=1, source_target_pairs={{0,8},{28,20},{8,16},{20,12},{16,24},{12,4},{1,9},{29,21},{9,17},{... | collective-permute-start | bytes 2359304 | tf_op jit(solution)/shard_map/ppermute | solution.py:117
  71.1 3.8 %collective-permute-done.5 = f32[64,3072]{1,0:T(8,128)S(1)} collective-permute-done((f32[64,3072]{1,0:T(8,128)S(1)}, f32[64,3072]{1,0:T(8,128)S(1)}, u32[]{:S(2)}, u32[]{:S(2)}) %collective-permute-start.5) | collective-permute-done | bytes 786464 | tf_op jit(solution)/shard_map/ppermute | solution.py:117
  74.9 8.4 %collective-permute-done.25 = f32[64,3072]{1,0:T(8,128)S(1)} collective-permute-done((f32[64,3072]{1,0:T(8,128)S(1)}, f32[64,3072]{1,0:T(8,128)S(1)}, u32[]{:S(2)}, u32[]{:S(2)}) %collective-permute-start.25) | collective-permute-done | bytes 786464 | tf_op jit(solution)/shard_map/ppermute | solution.py:117
  83.3 1.8 maximum_convert_fusion.1
  85.7 1.9 maximum_convert_fusion
  87.7 4.5 %collective-permute-start.27 = (bf16[64,3072]{1,0:T(8,128)(2,1)S(1)}, bf16[64,3072]{1,0:T(8,128)(2,1)S(1)}, u32[]{:S(2)}, u32[]{:S(2)}) collective-permute-start(bf16[64,3072]{1,0:T(8,128)(2,1)S(1)} %get-tuple-element.60), channel_id=1, source_target_pairs={{0,8},{28,20},{8,16},{20,12},{16,24},{12,4},{1,9},{29,21},{9,17},{... | collective-permute-start | bytes 1179656 | tf_op jit(solution)/shard_map/ppermute | solution.py:117
  92.2 5.3 %collective-permute-done.27 = bf16[64,3072]{1,0:T(8,128)(2,1)S(1)} collective-permute-done((bf16[64,3072]{1,0:T(8,128)(2,1)S(1)}, bf16[64,3072]{1,0:T(8,128)(2,1)S(1)}, u32[]{:S(2)}, u32[]{:S(2)}) %collective-permute-start.27) | collective-permute-done | bytes 393248 | tf_op jit(solution)/shard_map/ppermute | solution.py:117
  98.9 11.1 %collective-permute-start.7 = (bf16[64,3072]{1,0:T(8,128)(2,1)S(1)}, bf16[64,3072]{1,0:T(8,128)(2,1)S(1)}, u32[]{:S(2)}, u32[]{:S(2)}) collective-permute-start(bf16[64,3072]{1,0:T(8,128)(2,1)S(1)} %get-tuple-element.62), channel_id=1, source_target_pairs={{0,8},{28,20},{8,16},{20,12},{16,24},{12,4},{1,9},{29,21},{9,17},{... | collective-permute-start | bytes 1179656 | tf_op jit(solution)/shard_map/ppermute | solution.py:117
  110.1 4.6 %collective-permute-start.30 = (bf16[3,64,3072]{2,1,0:T(8,128)(2,1)S(1)}, bf16[3,64,3072]{2,1,0:T(8,128)(2,1)S(1)}, u32[]{:S(2)}, u32[]{:S(2)}) collective-permute-start(bf16[3,64,3072]{2,1,0:T(8,128)(2,1)S(1)} %pad_maximum_fusion.6), channel_id=1, source_target_pairs={{0,4},{4,0},{1,5},{5,1},{2,6},{6,2},{3,7},{7,3},{8,12},{12,8},{9,1... | collective-permute-start | bytes 3538952 | tf_op jit(solution)/shard_map/ppermute | solution.py:109
  116.9 19.0 %collective-permute-start.10 = (bf16[3,64,3072]{2,1,0:T(8,128)(2,1)S(1)}, bf16[3,64,3072]{2,1,0:T(8,128)(2,1)S(1)}, u32[]{:S(2)}, u32[]{:S(2)}) collective-permute-start(bf16[3,64,3072]{2,1,0:T(8,128)(2,1)S(1)} %pad_maximum_fusion.4), channel_id=1, source_target_pairs={{0,4},{4,0},{1,5},{5,1},{2,6},{6,2},{3,7},{7,3},{8,12},{12,8},{9,1... | collective-permute-start | bytes 3538952 | tf_op jit(solution)/shard_map/ppermute | solution.py:109
  136.5 1.8 convolution_convert_fusion
  138.3 1.6 collective-permute-start.31
  140.5 1.8 convolution_convert_fusion.1
  142.8 1.3 multiply_reduce_fusion
  144.4 3.2 %collective-permute-done.31 = bf16[256,1024]{1,0:T(8,128)(2,1)S(1)} collective-permute-done((bf16[256,1024]{1,0:T(8,128)(2,1)S(1)}, bf16[256,1024]{1,0:T(8,128)(2,1)S(1)}, u32[]{:S(2)}, u32[]{:S(2)}) %collective-permute-start.31) | collective-permute-done | bytes 524320 | tf_op jit(solution)/shard_map/ppermute | solution.py:159
  147.8 1.6 collective-permute-start.32
  149.4 6.6 %collective-permute-done.11 = bf16[256,1024]{1,0:T(8,128)(2,1)S(1)} collective-permute-done((bf16[256,1024]{1,0:T(8,128)(2,1)S(1)}, bf16[256,1024]{1,0:T(8,128)(2,1)S(1)}, u32[]{:S(2)}, u32[]{:S(2)}) %collective-permute-start.11) | collective-permute-done | bytes 524320 | tf_op jit(solution)/shard_map/ppermute | solution.py:159
  156.2 1.6 collective-permute-start.12
  158.8 6.6 %collective-permute-done.12 = bf16[256,1024]{1,0:T(8,128)(2,1)S(1)} collective-permute-done((bf16[256,1024]{1,0:T(8,128)(2,1)S(1)}, bf16[256,1024]{1,0:T(8,128)(2,1)S(1)}, u32[]{:S(2)}, u32[]{:S(2)}) %collective-permute-start.12) | collective-permute-done | bytes 524320 | tf_op jit(solution)/shard_map/ppermute | solution.py:159
  165.8 1.8 fusion
  168.3 1.8 fusion.1
  171.2 2.0 collective-permute-start.14
  173.9 1.8 collective-permute-start.34
  175.6 2.9 collective-permute-done.14
  178.7 4.6 %collective-permute-start.15 = (bf16[64,3072]{1,0:T(8,128)(2,1)S(1)}, bf16[64,3072]{1,0:T(8,128)(2,1)S(1)}, u32[]{:S(2)}, u32[]{:S(2)}) collective-permute-start(bf16[64,3072]{1,0:T(8,128)(2,1)S(1)} %fusion.28), channel_id=1, source_target_pairs={{0,8},{28,20},{8,16},{20,12},{1,9},{29,21},{9,17},{21,13},{2,10},{... | collective-permute-start | bytes 1179656 | tf_op jit(solution)/shard_map/ppermute | solution.py:117
  183.5 3.8 %collective-permute-start.35 = (bf16[64,3072]{1,0:T(8,128)(2,1)S(1)}, bf16[64,3072]{1,0:T(8,128)(2,1)S(1)}, u32[]{:S(2)}, u32[]{:S(2)}) collective-permute-start(bf16[64,3072]{1,0:T(8,128)(2,1)S(1)} %fusion.20), channel_id=1, source_target_pairs={{0,8},{28,20},{8,16},{20,12},{1,9},{29,21},{9,17},{21,13},{2,10},{... | collective-permute-start | bytes 1179656 | tf_op jit(solution)/shard_map/ppermute | solution.py:117
  187.3 1.0 collective-permute-done.15
  188.5 4.7 %collective-permute-start.16 = (bf16[64,3072]{1,0:T(8,128)(2,1)S(1)}, bf16[64,3072]{1,0:T(8,128)(2,1)S(1)}, u32[]{:S(2)}, u32[]{:S(2)}) collective-permute-start(bf16[64,3072]{1,0:T(8,128)(2,1)S(1)} %fusion.30), channel_id=1, source_target_pairs={{0,8},{28,20},{8,16},{20,12},{16,24},{12,4},{1,9},{29,21},{9,17},{... | collective-permute-start | bytes 1179656 | tf_op jit(solution)/shard_map/ppermute | solution.py:117
  193.3 3.8 %collective-permute-start.36 = (bf16[64,3072]{1,0:T(8,128)(2,1)S(1)}, bf16[64,3072]{1,0:T(8,128)(2,1)S(1)}, u32[]{:S(2)}, u32[]{:S(2)}) collective-permute-start(bf16[64,3072]{1,0:T(8,128)(2,1)S(1)} %fusion.22), channel_id=1, source_target_pairs={{0,8},{28,20},{8,16},{20,12},{16,24},{12,4},{1,9},{29,21},{9,17},{... | collective-permute-start | bytes 1179656 | tf_op jit(solution)/shard_map/ppermute | solution.py:117
  197.1 1.3 collective-permute-done.16
  198.4 3.3 %collective-permute-start.17 = (bf16[64,3072]{1,0:T(8,128)(2,1)S(1)}, bf16[64,3072]{1,0:T(8,128)(2,1)S(1)}, u32[]{:S(2)}, u32[]{:S(2)}) collective-permute-start(bf16[64,3072]{1,0:T(8,128)(2,1)S(1)} %collective-permute-done.16), channel_id=1, source_target_pairs={{0,4},{4,0},{1,5},{5,1},{2,6},{6,2},{3,7},{7,3},{8,12},{12,8},{9,1... | collective-permute-start | bytes 1179656 | tf_op jit(solution)/shard_map/ppermute | solution.py:109
  201.7 1.0 collective-permute-done.36
  202.6 3.3 %collective-permute-start.37 = (bf16[64,3072]{1,0:T(8,128)(2,1)S(1)}, bf16[64,3072]{1,0:T(8,128)(2,1)S(1)}, u32[]{:S(2)}, u32[]{:S(2)}) collective-permute-start(bf16[64,3072]{1,0:T(8,128)(2,1)S(1)} %collective-permute-done.36), channel_id=1, source_target_pairs={{0,4},{4,0},{1,5},{5,1},{2,6},{6,2},{3,7},{7,3},{8,12},{12,8},{9,1... | collective-permute-start | bytes 1179656 | tf_op jit(solution)/shard_map/ppermute | solution.py:109
  206.1 1.1 collective-permute-done.37
  207.5 3.8 %collective-permute-start.38 = (bf16[64,3072]{1,0:T(8,128)(2,1)S(1)}, bf16[64,3072]{1,0:T(8,128)(2,1)S(1)}, u32[]{:S(2)}, u32[]{:S(2)}) collective-permute-start(bf16[64,3072]{1,0:T(8,128)(2,1)S(1)} %fusion.25), channel_id=1, source_target_pairs={{0,8},{28,20},{8,16},{20,12},{16,24},{12,4},{1,9},{29,21},{9,17},{... | collective-permute-start | bytes 1179656 | tf_op jit(solution)/shard_map/ppermute | solution.py:117
  211.3 5.3 %collective-permute-done.38 = bf16[64,3072]{1,0:T(8,128)(2,1)S(1)} collective-permute-done((bf16[64,3072]{1,0:T(8,128)(2,1)S(1)}, bf16[64,3072]{1,0:T(8,128)(2,1)S(1)}, u32[]{:S(2)}, u32[]{:S(2)}) %collective-permute-start.38) | collective-permute-done | bytes 393248 | tf_op jit(solution)/shard_map/ppermute | solution.py:117
  217.2 7.1 %collective-permute-start.18 = (bf16[64,3072]{1,0:T(8,128)(2,1)S(1)}, bf16[64,3072]{1,0:T(8,128)(2,1)S(1)}, u32[]{:S(2)}, u32[]{:S(2)}) collective-permute-start(bf16[64,3072]{1,0:T(8,128)(2,1)S(1)} %fusion.33), channel_id=1, source_target_pairs={{0,8},{28,20},{8,16},{20,12},{16,24},{12,4},{1,9},{29,21},{9,17},{... | collective-permute-start | bytes 1179656 | tf_op jit(solution)/shard_map/ppermute | solution.py:117
  225.1 4.5 %collective-permute-done.18 = bf16[64,3072]{1,0:T(8,128)(2,1)S(1)} collective-permute-done((bf16[64,3072]{1,0:T(8,128)(2,1)S(1)}, bf16[64,3072]{1,0:T(8,128)(2,1)S(1)}, u32[]{:S(2)}, u32[]{:S(2)}) %collective-permute-start.18) | collective-permute-done | bytes 393248 | tf_op jit(solution)/shard_map/ppermute | solution.py:117
  230.4 3.6 %collective-permute-start.41 = (bf16[3,64,3072]{2,1,0:T(8,128)(2,1)S(1)}, bf16[3,64,3072]{2,1,0:T(8,128)(2,1)S(1)}, u32[]{:S(2)}, u32[]{:S(2)}) collective-permute-start(bf16[3,64,3072]{2,1,0:T(8,128)(2,1)S(1)} %pad_maximum_fusion.7), channel_id=1, source_target_pairs={{0,4},{4,0},{1,5},{5,1},{2,6},{6,2},{3,7},{7,3},{8,12},{12,8},{9,1... | collective-permute-start | bytes 3538952 | tf_op jit(solution)/shard_map/ppermute | solution.py:109
  234.9 12.2 %collective-permute-start.21 = (bf16[3,64,3072]{2,1,0:T(8,128)(2,1)S(1)}, bf16[3,64,3072]{2,1,0:T(8,128)(2,1)S(1)}, u32[]{:S(2)}, u32[]{:S(2)}) collective-permute-start(bf16[3,64,3072]{2,1,0:T(8,128)(2,1)S(1)} %pad_maximum_fusion.5), channel_id=1, source_target_pairs={{0,4},{4,0},{1,5},{5,1},{2,6},{6,2},{3,7},{7,3},{8,12},{12,8},{9,1... | collective-permute-start | bytes 3538952 | tf_op jit(solution)/shard_map/ppermute | solution.py:109
  248.2 3.4 %adam.8 = (bf16[3072,1024]{1,0:T(8,128)(2,1)}, bf16[3072,1024]{1,0:T(8,128)(2,1)}, bf16[3072,1024]{1,0:T(8,128)(2,1)}) custom-call(bf16[256,3072]{1,0:T(8,128)(2,1)S(1)} %bitcast.166, bf16[256,3072]{1,0:T(8,128)(2,1)S(1)} %bitcast.159, bf16[256,1024]{1,0:T(8,128)(2,1)S(1)} %fusion.37.refs_2_, bf16[256,1024]{1,0:T(8,128)(2,1)S(1)} %get-tuple-element.64.refs_3_, ...), custom_call_target="tpu_custom_call" | custom-call | flops 536870912 | bytes 6291456 | tf_op jit(solution)/shard_map/adam/pallas_call | solution.py:82
  251.5 3.3 %adam.9 = (bf16[3072,1024]{1,0:T(8,128)(2,1)}, bf16[3072,1024]{1,0:T(8,128)(2,1)}, bf16[3072,1024]{1,0:T(8,128)(2,1)}) custom-call(bf16[256,3072]{1,0:T(8,128)(2,1)S(1)} %bitcast.167, bf16[256,3072]{1,0:T(8,128)(2,1)S(1)} %bitcast.160, bf16[256,1024]{1,0:T(8,128)(2,1)S(1)} %fusion.37.refs_2_, ...), custom_call_target="tpu_custom_call", output_to_operand_aliasing={{0}: (8, {}), {1}: (9, {}), {2}: (10, {})} | custom-call | flops 536870912 | bytes 6291456 | tf_op jit(solution)/shard_map/adam/pallas_call | solution.py:82
  254.9 3.3 %adam.10 = (bf16[3072,1024]{1,0:T(8,128)(2,1)}, bf16[3072,1024]{1,0:T(8,128)(2,1)}, bf16[3072,1024]{1,0:T(8,128)(2,1)}) custom-call(bf16[256,3072]{1,0:T(8,128)(2,1)S(1)} %bitcast.168, bf16[256,3072]{1,0:T(8,128)(2,1)S(1)} %bitcast.161, bf16[256,1024]{1,0:T(8,128)(2,1)S(1)} %fusion.37.refs_2_, ...), custom_call_target="tpu_custom_call", output_to_operand_aliasing={{0}: (8, {}), {1}: (9, {}), {2}: (10, {})} | custom-call | flops 536870912 | bytes 6291456 | tf_op jit(solution)/shard_map/adam/pallas_call | solution.py:82
  258.2 3.3 %adam.11 = (bf16[3072,1024]{1,0:T(8,128)(2,1)}, bf16[3072,1024]{1,0:T(8,128)(2,1)}, bf16[3072,1024]{1,0:T(8,128)(2,1)}) custom-call(bf16[256,3072]{1,0:T(8,128)(2,1)S(1)} %bitcast.169, bf16[256,3072]{1,0:T(8,128)(2,1)S(1)} %bitcast.162, bf16[256,1024]{1,0:T(8,128)(2,1)S(1)} %fusion.37.refs_2_, ...), custom_call_target="tpu_custom_call", output_to_operand_aliasing={{0}: (8, {}), {1}: (9, {}), {2}: (10, {})} | custom-call | flops 536870912 | bytes 6291456 | tf_op jit(solution)/shard_map/adam/pallas_call | solution.py:82
  261.5 3.3 %adam.12 = (bf16[3072,1024]{1,0:T(8,128)(2,1)}, bf16[3072,1024]{1,0:T(8,128)(2,1)}, bf16[3072,1024]{1,0:T(8,128)(2,1)}) custom-call(bf16[256,3072]{1,0:T(8,128)(2,1)S(1)} %bitcast.170, bf16[256,3072]{1,0:T(8,128)(2,1)S(1)} %bitcast.163, bf16[256,1024]{1,0:T(8,128)(2,1)S(1)} %fusion.37.refs_2_, ...), custom_call_target="tpu_custom_call", output_to_operand_aliasing={{0}: (8, {}), {1}: (9, {}), {2}: (10, {})} | custom-call | flops 536870912 | bytes 6291456 | tf_op jit(solution)/shard_map/adam/pallas_call | solution.py:82
  264.9 3.3 %adam.13 = (bf16[3072,1024]{1,0:T(8,128)(2,1)}, bf16[3072,1024]{1,0:T(8,128)(2,1)}, bf16[3072,1024]{1,0:T(8,128)(2,1)}) custom-call(bf16[256,3072]{1,0:T(8,128)(2,1)S(1)} %bitcast.171, bf16[256,3072]{1,0:T(8,128)(2,1)S(1)} %bitcast.164, bf16[256,1024]{1,0:T(8,128)(2,1)S(1)} %fusion.37.refs_2_, ...), custom_call_target="tpu_custom_call", output_to_operand_aliasing={{0}: (8, {}), {1}: (9, {}), {2}: (10, {})} | custom-call | flops 536870912 | bytes 6291456 | tf_op jit(solution)/shard_map/adam/pallas_call | solution.py:82
  271.6 2.8 copy-done.2
  274.4 13.1 %adam.7 = (bf16[1024,3072]{1,0:T(8,128)(2,1)}, bf16[1024,3072]{1,0:T(8,128)(2,1)}, bf16[1024,3072]{1,0:T(8,128)(2,1)}) custom-call(bf16[256,1024]{1,0:T(8,128)(2,1)S(1)} %bitcast.173, bf16[256,1024]{1,0:T(8,128)(2,1)S(1)} %bitcast.183, bf16[256,3072]{1,0:T(8,128)(2,1)S(1)} %bitcast.175, bf16[256,3072]{1,0:T(8,128)(2,1)S(1)} %bitcast.174, ...), custom_call_target="tpu_custom_call" | custom-call | flops 3221225472 | bytes 37748736 | tf_op jit(solution)/shard_map/adam/pallas_call | solution.py:82
  (134 shorter events, 21.9 us)
Async XLA Ops:
  0.6 1.1 copy-start
  2.4 10.2 %collective-permute-start = (bf16[4,32,1024]{2,1,0:T(8,128)(2,1)S(1)}, bf16[4,32,1024]{2,1,0:T(8,128)(2,1)S(1)}, u32[]{:S(2)}, u32[]{:S(2)}) collective-permute-start(bf16[4,32,1024]{2,1,0:T(8,128)(2,1)S(1)} %get-tuple-element.70), channel_id=1, source_target_pairs={{0,1},{1,0},{2,3},{3,2},{4,5},{5,4},{6,7},{7,6},{8,9},{9,8},{10,11... | collective-permute-start | bytes 786440 | tf_op jit(solution)/shard_map/ppermute | solution.py:200
  5.5 11.9 %collective-permute-start.1 = (bf16[4,32,1024]{2,1,0:T(8,128)(2,1)S(1)}, bf16[4,32,1024]{2,1,0:T(8,128)(2,1)S(1)}, u32[]{:S(2)}, u32[]{:S(2)}) collective-permute-start(bf16[4,32,1024]{2,1,0:T(8,128)(2,1)S(1)} %get-tuple-element.69), channel_id=1, source_target_pairs={{0,1},{1,0},{2,3},{3,2},{4,5},{5,4},{6,7},{7,6},{8,9},{9,8},{10,11... | collective-permute-start | bytes 786440 | tf_op jit(solution)/shard_map/ppermute | solution.py:200
  17.4 4.9 %slice-start.6 = ((s8[6291456]{0:T(1024)(128)(4,1)}), s8[4194304]{0:T(1024)(128)(4,1)S(1)}, s32[]{:S(2)}) async-start(s8[6291456]{0:T(1024)(128)(4,1)} %bitcast.176), calls=%async_computation.6 | async-start | bytes 8388608
  17.4 4.9 %slice-start.7 = ((s8[6291456]{0:T(1024)(128)(4,1)}), s8[2097152]{0:T(1024)(128)(4,1)S(1)}, s32[]{:S(2)}) async-start(s8[6291456]{0:T(1024)(128)(4,1)} %bitcast.176), calls=%async_computation.7 | async-start | bytes 4194304
  22.1 35.9 %copy-start.3 = (f32[256,3072]{1,0:T(8,128)}, f32[256,3072]{1,0:T(8,128)S(1)}, u32[]{:S(2)}) copy-start(f32[256,3072]{1,0:T(8,128)S(1)} %fusion.46) | copy-start | bytes 9437188
  22.1 5.7 %collective-permute-start.2 = (f32[4,64,3072]{2,1,0:T(8,128)S(1)}, f32[4,64,3072]{2,1,0:T(8,128)S(1)}, u32[]{:S(2)}, u32[]{:S(2)}) collective-permute-start(f32[4,64,3072]{2,1,0:T(8,128)S(1)} %bitcast.192), channel_id=1, source_target_pairs={{0,4},{4,0},{1,5},{5,1},{2,6},{6,2},{3,7},{7,3},{8,12},{12,8},{9,1... | collective-permute-start | bytes 9437192 | tf_op jit(solution)/shard_map/ppermute | solution.py:109
  24.2 42.3 %copy-start.5 = (f32[256,3072]{1,0:T(8,128)}, f32[256,3072]{1,0:T(8,128)S(1)}, u32[]{:S(2)}) copy-start(f32[256,3072]{1,0:T(8,128)S(1)} %fusion.47) | copy-start | bytes 9437188
  24.2 8.2 %collective-permute-start.22 = (f32[4,64,3072]{2,1,0:T(8,128)S(1)}, f32[4,64,3072]{2,1,0:T(8,128)S(1)}, u32[]{:S(2)}, u32[]{:S(2)}) collective-permute-start(f32[4,64,3072]{2,1,0:T(8,128)S(1)} %bitcast.193), channel_id=1, source_target_pairs={{0,4},{4,0},{1,5},{5,1},{2,6},{6,2},{3,7},{7,3},{8,12},{12,8},{9,1... | collective-permute-start | bytes 9437192 | tf_op jit(solution)/shard_map/ppermute | solution.py:109
  27.9 30.2 %copy-start.4 = (f32[4,64,3072]{2,1,0:T(8,128)}, f32[4,64,3072]{2,1,0:T(8,128)S(1)}, u32[]{:S(2)}) copy-start(f32[4,64,3072]{2,1,0:T(8,128)S(1)} %collective-permute-done.2) | copy-start | bytes 9437188
  28.0 13.2 %collective-permute-start.3 = (f32[64,3072]{1,0:T(8,128)S(1)}, f32[64,3072]{1,0:T(8,128)S(1)}, u32[]{:S(2)}, u32[]{:S(2)}) collective-permute-start(f32[64,3072]{1,0:T(8,128)S(1)} %fusion.10), channel_id=1, source_target_pairs={{0,8},{28,20},{1,9},{29,21},{2,10},{30,22},{3,11},{31,23}} | collective-permute-start | bytes 2359304 | tf_op jit(solution)/shard_map/ppermute | solution.py:117
  32.4 34.1 %copy-start.6 = (f32[4,64,3072]{2,1,0:T(8,128)}, f32[4,64,3072]{2,1,0:T(8,128)S(1)}, u32[]{:S(2)}) copy-start(f32[4,64,3072]{2,1,0:T(8,128)S(1)} %collective-permute-done.22) | copy-start | bytes 9437188
  32.5 17.1 %collective-permute-start.23 = (f32[64,3072]{1,0:T(8,128)S(1)}, f32[64,3072]{1,0:T(8,128)S(1)}, u32[]{:S(2)}, u32[]{:S(2)}) collective-permute-start(f32[64,3072]{1,0:T(8,128)S(1)} %fusion.2), channel_id=1, source_target_pairs={{0,8},{28,20},{1,9},{29,21},{2,10},{30,22},{3,11},{31,23}} | collective-permute-start | bytes 2359304 | tf_op jit(solution)/shard_map/ppermute | solution.py:117
  41.3 16.7 %collective-permute-start.4 = (f32[64,3072]{1,0:T(8,128)S(1)}, f32[64,3072]{1,0:T(8,128)S(1)}, u32[]{:S(2)}, u32[]{:S(2)}) collective-permute-start(f32[64,3072]{1,0:T(8,128)S(1)} %fusion.12), channel_id=1, source_target_pairs={{0,8},{28,20},{8,16},{20,12},{1,9},{29,21},{9,17},{21,13},{2,10},{... | collective-permute-start | bytes 2359304 | tf_op jit(solution)/shard_map/ppermute | solution.py:117
  49.8 16.7 %collective-permute-start.24 = (f32[64,3072]{1,0:T(8,128)S(1)}, f32[64,3072]{1,0:T(8,128)S(1)}, u32[]{:S(2)}, u32[]{:S(2)}) collective-permute-start(f32[64,3072]{1,0:T(8,128)S(1)} %fusion.4), channel_id=1, source_target_pairs={{0,8},{28,20},{8,16},{20,12},{1,9},{29,21},{9,17},{21,13},{2,10},{... | collective-permute-start | bytes 2359304 | tf_op jit(solution)/shard_map/ppermute | solution.py:117
  58.2 25.1 %copy-start.8 = (f32[6144]{0:T(1024)S(1)}, f32[6144]{0:T(1024)}, u32[]{:S(2)}) copy-start(f32[6144]{0:T(1024)} %param.12) | copy-start | bytes 73732
  58.2 16.7 %collective-permute-start.5 = (f32[64,3072]{1,0:T(8,128)S(1)}, f32[64,3072]{1,0:T(8,128)S(1)}, u32[]{:S(2)}, u32[]{:S(2)}) collective-permute-start(f32[64,3072]{1,0:T(8,128)S(1)} %fusion.14), channel_id=1, source_target_pairs={{0,8},{28,20},{8,16},{20,12},{16,24},{12,4},{1,9},{29,21},{9,17},{... | collective-permute-start | bytes 2359304 | tf_op jit(solution)/shard_map/ppermute | solution.py:117
  66.6 16.7 %collective-permute-start.25 = (f32[64,3072]{1,0:T(8,128)S(1)}, f32[64,3072]{1,0:T(8,128)S(1)}, u32[]{:S(2)}, u32[]{:S(2)}) collective-permute-start(f32[64,3072]{1,0:T(8,128)S(1)} %fusion.6), channel_id=1, source_target_pairs={{0,8},{28,20},{8,16},{20,12},{16,24},{12,4},{1,9},{29,21},{9,17},{... | collective-permute-start | bytes 2359304 | tf_op jit(solution)/shard_map/ppermute | solution.py:117
  74.9 8.4 %collective-permute-start.6 = (f32[64,3072]{1,0:T(8,128)S(1)}, f32[64,3072]{1,0:T(8,128)}, u32[]{:S(2)}, u32[]{:S(2)}) collective-permute-start(f32[64,3072]{1,0:T(8,128)S(1)} %collective-permute-done.5), channel_id=1, source_target_pairs={{0,4},{4,0},{1,5},{5,1},{2,6},{6,2},{3,7},{7,3},{8,12},{12,8},{9,1... | collective-permute-start | bytes 2359304 | tf_op jit(solution)/shard_map/ppermute | solution.py:109
  83.3 2.4 collective-permute-start.26
  85.7 50.8 %slice-start = ((s8[6291456]{0:T(1024)(128)(4,1)}), s8[4194304]{0:T(1024)(128)(4,1)S(1)}, s32[]{:S(2)}) async-start(s8[6291456]{0:T(1024)(128)(4,1)} %bitcast.152), calls=%async_computation | async-start | bytes 8388608
  87.7 9.8 %collective-permute-start.27 = (bf16[64,3072]{1,0:T(8,128)(2,1)S(1)}, bf16[64,3072]{1,0:T(8,128)(2,1)S(1)}, u32[]{:S(2)}, u32[]{:S(2)}) collective-permute-start(bf16[64,3072]{1,0:T(8,128)(2,1)S(1)} %get-tuple-element.60), channel_id=1, source_target_pairs={{0,8},{28,20},{8,16},{20,12},{16,24},{12,4},{1,9},{29,21},{9,17},{... | collective-permute-start | bytes 1179656 | tf_op jit(solution)/shard_map/ppermute | solution.py:117
  97.5 0.7 collective-permute-start.28
  98.2 11.8 %collective-permute-start.29 = (bf16[64,3072]{1,0:T(8,128)(2,1)S(1)}, bf16[64,3072]{1,0:T(8,128)(2,1)S(1)}, u32[]{:S(2)}, u32[]{:S(2)}) collective-permute-start(bf16[64,3072]{1,0:T(8,128)(2,1)S(1)} %collective-permute-done.28), channel_id=1, source_target_pairs={{16,24},{12,4},{17,25},{13,5},{18,26},{14,6},{19,27},{15,7}} | collective-permute-start | bytes 1179656 | tf_op jit(solution)/shard_map/ppermute | solution.py:117
  98.9 16.3 %collective-permute-start.7 = (bf16[64,3072]{1,0:T(8,128)(2,1)S(1)}, bf16[64,3072]{1,0:T(8,128)(2,1)S(1)}, u32[]{:S(2)}, u32[]{:S(2)}) collective-permute-start(bf16[64,3072]{1,0:T(8,128)(2,1)S(1)} %get-tuple-element.62), channel_id=1, source_target_pairs={{0,8},{28,20},{8,16},{20,12},{16,24},{12,4},{1,9},{29,21},{9,17},{... | collective-permute-start | bytes 1179656 | tf_op jit(solution)/shard_map/ppermute | solution.py:117
  110.1 25.9 %collective-permute-start.30 = (bf16[3,64,3072]{2,1,0:T(8,128)(2,1)S(1)}, bf16[3,64,3072]{2,1,0:T(8,128)(2,1)S(1)}, u32[]{:S(2)}, u32[]{:S(2)}) collective-permute-start(bf16[3,64,3072]{2,1,0:T(8,128)(2,1)S(1)} %pad_maximum_fusion.6), channel_id=1, source_target_pairs={{0,4},{4,0},{1,5},{5,1},{2,6},{6,2},{3,7},{7,3},{8,12},{12,8},{9,1... | collective-permute-start | bytes 3538952 | tf_op jit(solution)/shard_map/ppermute | solution.py:109
  115.2 0.7 collective-permute-start.8
  115.9 0.9 collective-permute-start.9
  116.8 19.8 %slice-start.1 = ((s8[6291456]{0:T(1024)(128)(4,1)}), s8[2097152]{0:T(1024)(128)(4,1)S(1)}, s32[]{:S(2)}) async-start(s8[6291456]{0:T(1024)(128)(4,1)} %bitcast.152), calls=%async_computation.1 | async-start | bytes 4194304
  116.9 23.0 %collective-permute-start.10 = (bf16[3,64,3072]{2,1,0:T(8,128)(2,1)S(1)}, bf16[3,64,3072]{2,1,0:T(8,128)(2,1)S(1)}, u32[]{:S(2)}, u32[]{:S(2)}) collective-permute-start(bf16[3,64,3072]{2,1,0:T(8,128)(2,1)S(1)} %pad_maximum_fusion.4), channel_id=1, source_target_pairs={{0,4},{4,0},{1,5},{5,1},{2,6},{6,2},{3,7},{7,3},{8,12},{12,8},{9,1... | collective-permute-start | bytes 3538952 | tf_op jit(solution)/shard_map/ppermute | solution.py:109
  138.3 9.2 %collective-permute-start.31 = (bf16[256,1024]{1,0:T(8,128)(2,1)S(1)}, bf16[256,1024]{1,0:T(8,128)(2,1)S(1)}, u32[]{:S(2)}, u32[]{:S(2)}) collective-permute-start(bf16[256,1024]{1,0:T(8,128)(2,1)S(1)} %convolution_convert_fusion), channel_id=1, source_target_pairs={{0,1},{1,0},{2,3},{3,2},{4,6},{5,7},{6,4},{7,5},{8,9},{9,8},{10,11... | collective-permute-start | bytes 1572872 | tf_op jit(solution)/shard_map/ppermute | solution.py:159
  142.2 13.8 %collective-permute-start.11 = (bf16[256,1024]{1,0:T(8,128)(2,1)S(1)}, bf16[256,1024]{1,0:T(8,128)(2,1)S(1)}, u32[]{:S(2)}, u32[]{:S(2)}) collective-permute-start(bf16[256,1024]{1,0:T(8,128)(2,1)S(1)} %convolution_convert_fusion.1), channel_id=1, source_target_pairs={{0,1},{1,0},{2,3},{3,2},{4,6},{5,7},{6,4},{7,5},{8,9},{9,8},{10,11... | collective-permute-start | bytes 1572872 | tf_op jit(solution)/shard_map/ppermute | solution.py:159
  147.8 10.9 %collective-permute-start.32 = (bf16[256,1024]{1,0:T(8,128)(2,1)S(1)}, bf16[256,1024]{1,0:T(8,128)(2,1)S(1)}, u32[]{:S(2)}, u32[]{:S(2)}) collective-permute-start(bf16[256,1024]{1,0:T(8,128)(2,1)S(1)} %add_convert_fusion), channel_id=1, source_target_pairs={{0,2},{1,3},{2,0},{3,1},{4,5},{5,4},{6,7},{7,6},{8,10},{9,11},{10,... | collective-permute-start | bytes 1572872 | tf_op jit(solution)/shard_map/ppermute | solution.py:159
  156.2 9.3 %copy-start.7 = (f32[1024]{0:T(1024)S(1)}, f32[1024]{0:T(1024)}, u32[]{:S(2)}) copy-start(f32[1024]{0:T(1024)} %param.13) | copy-start | bytes 12292
  156.2 9.2 %collective-permute-start.12 = (bf16[256,1024]{1,0:T(8,128)(2,1)S(1)}, bf16[256,1024]{1,0:T(8,128)(2,1)S(1)}, u32[]{:S(2)}, u32[]{:S(2)}) collective-permute-start(bf16[256,1024]{1,0:T(8,128)(2,1)S(1)} %add_convert_fusion.1), channel_id=1, source_target_pairs={{0,2},{1,3},{2,0},{3,1},{4,5},{5,4},{6,7},{7,6},{8,10},{9,11},{10,... | collective-permute-start | bytes 1572872 | tf_op jit(solution)/shard_map/ppermute | solution.py:159
  167.6 3.5 %collective-permute-start.13 = (bf16[4,64,3072]{2,1,0:T(8,128)(2,1)S(1)}, bf16[4,64,3072]{2,1,0:T(8,128)(2,1)S(1)}, u32[]{:S(2)}, u32[]{:S(2)}) collective-permute-start(bf16[4,64,3072]{2,1,0:T(8,128)(2,1)S(1)} %bitcast.218), channel_id=1, source_target_pairs={{0,4},{4,0},{1,5},{5,1},{2,6},{6,2},{3,7},{7,3},{8,12},{12,8},{9,1... | collective-permute-start | bytes 4718600 | tf_op jit(solution)/shard_map/ppermute | solution.py:109
  170.2 3.6 %collective-permute-start.33 = (bf16[4,64,3072]{2,1,0:T(8,128)(2,1)S(1)}, bf16[4,64,3072]{2,1,0:T(8,128)(2,1)S(1)}, u32[]{:S(2)}, u32[]{:S(2)}) collective-permute-start(bf16[4,64,3072]{2,1,0:T(8,128)(2,1)S(1)} %bitcast.219), channel_id=1, source_target_pairs={{0,4},{4,0},{1,5},{5,1},{2,6},{6,2},{3,7},{7,3},{8,12},{12,8},{9,1... | collective-permute-start | bytes 4718600 | tf_op jit(solution)/shard_map/ppermute | solution.py:109
  171.1 77.0 %slice-start.4 = ((s8[6291456]{0:T(1024)(128)(4,1)}), s8[4194304]{0:T(1024)(128)(4,1)S(1)}, s32[]{:S(2)}) async-start(s8[6291456]{0:T(1024)(128)(4,1)} %bitcast.156), calls=%async_computation.4 | async-start | bytes 8388608
  171.2 7.3 %collective-permute-start.14 = (bf16[64,3072]{1,0:T(8,128)(2,1)S(1)}, bf16[64,3072]{1,0:T(8,128)(2,1)S(1)}, u32[]{:S(2)}, u32[]{:S(2)}) collective-permute-start(bf16[64,3072]{1,0:T(8,128)(2,1)S(1)} %fusion.26), channel_id=1, source_target_pairs={{0,8},{28,20},{1,9},{29,21},{2,10},{30,22},{3,11},{31,23}} | collective-permute-start | bytes 1179656 | tf_op jit(solution)/shard_map/ppermute | solution.py:117
  173.9 9.4 %collective-permute-start.34 = (bf16[64,3072]{1,0:T(8,128)(2,1)S(1)}, bf16[64,3072]{1,0:T(8,128)(2,1)S(1)}, u32[]{:S(2)}, u32[]{:S(2)}) collective-permute-start(bf16[64,3072]{1,0:T(8,128)(2,1)S(1)} %fusion.18), channel_id=1, source_target_pairs={{0,8},{28,20},{1,9},{29,21},{2,10},{30,22},{3,11},{31,23}} | collective-permute-start | bytes 1179656 | tf_op jit(solution)/shard_map/ppermute | solution.py:117
  178.7 9.7 %collective-permute-start.15 = (bf16[64,3072]{1,0:T(8,128)(2,1)S(1)}, bf16[64,3072]{1,0:T(8,128)(2,1)S(1)}, u32[]{:S(2)}, u32[]{:S(2)}) collective-permute-start(bf16[64,3072]{1,0:T(8,128)(2,1)S(1)} %fusion.28), channel_id=1, source_target_pairs={{0,8},{28,20},{8,16},{20,12},{1,9},{29,21},{9,17},{21,13},{2,10},{... | collective-permute-start | bytes 1179656 | tf_op jit(solution)/shard_map/ppermute | solution.py:117
  183.5 9.7 %collective-permute-start.35 = (bf16[64,3072]{1,0:T(8,128)(2,1)S(1)}, bf16[64,3072]{1,0:T(8,128)(2,1)S(1)}, u32[]{:S(2)}, u32[]{:S(2)}) collective-permute-start(bf16[64,3072]{1,0:T(8,128)(2,1)S(1)} %fusion.20), channel_id=1, source_target_pairs={{0,8},{28,20},{8,16},{20,12},{1,9},{29,21},{9,17},{21,13},{2,10},{... | collective-permute-start | bytes 1179656 | tf_op jit(solution)/shard_map/ppermute | solution.py:117
  188.3 59.8 %slice-start.2 = ((s8[6291456]{0:T(1024)(128)(4,1)}), s8[4194304]{0:T(1024)(128)(4,1)S(1)}, s32[]{:S(2)}) async-start(s8[6291456]{0:T(1024)(128)(4,1)} %bitcast.154), calls=%async_computation.2 | async-start | bytes 8388608
  188.5 9.9 %collective-permute-start.16 = (bf16[64,3072]{1,0:T(8,128)(2,1)S(1)}, bf16[64,3072]{1,0:T(8,128)(2,1)S(1)}, u32[]{:S(2)}, u32[]{:S(2)}) collective-permute-start(bf16[64,3072]{1,0:T(8,128)(2,1)S(1)} %fusion.30), channel_id=1, source_target_pairs={{0,8},{28,20},{8,16},{20,12},{16,24},{12,4},{1,9},{29,21},{9,17},{... | collective-permute-start | bytes 1179656 | tf_op jit(solution)/shard_map/ppermute | solution.py:117
  193.3 9.3 %collective-permute-start.36 = (bf16[64,3072]{1,0:T(8,128)(2,1)S(1)}, bf16[64,3072]{1,0:T(8,128)(2,1)S(1)}, u32[]{:S(2)}, u32[]{:S(2)}) collective-permute-start(bf16[64,3072]{1,0:T(8,128)(2,1)S(1)} %fusion.22), channel_id=1, source_target_pairs={{0,8},{28,20},{8,16},{20,12},{16,24},{12,4},{1,9},{29,21},{9,17},{... | collective-permute-start | bytes 1179656 | tf_op jit(solution)/shard_map/ppermute | solution.py:117
  198.4 7.5 %collective-permute-start.17 = (bf16[64,3072]{1,0:T(8,128)(2,1)S(1)}, bf16[64,3072]{1,0:T(8,128)(2,1)S(1)}, u32[]{:S(2)}, u32[]{:S(2)}) collective-permute-start(bf16[64,3072]{1,0:T(8,128)(2,1)S(1)} %collective-permute-done.16), channel_id=1, source_target_pairs={{0,4},{4,0},{1,5},{5,1},{2,6},{6,2},{3,7},{7,3},{8,12},{12,8},{9,1... | collective-permute-start | bytes 1179656 | tf_op jit(solution)/shard_map/ppermute | solution.py:109
  202.6 4.6 %collective-permute-start.37 = (bf16[64,3072]{1,0:T(8,128)(2,1)S(1)}, bf16[64,3072]{1,0:T(8,128)(2,1)S(1)}, u32[]{:S(2)}, u32[]{:S(2)}) collective-permute-start(bf16[64,3072]{1,0:T(8,128)(2,1)S(1)} %collective-permute-done.36), channel_id=1, source_target_pairs={{0,4},{4,0},{1,5},{5,1},{2,6},{6,2},{3,7},{7,3},{8,12},{12,8},{9,1... | collective-permute-start | bytes 1179656 | tf_op jit(solution)/shard_map/ppermute | solution.py:109
  205.9 42.2 %slice-start.5 = ((s8[6291456]{0:T(1024)(128)(4,1)}), s8[2097152]{0:T(1024)(128)(4,1)S(1)}, s32[]{:S(2)}) async-start(s8[6291456]{0:T(1024)(128)(4,1)} %bitcast.156), calls=%async_computation.5 | async-start | bytes 4194304
  207.2 40.9 %slice-start.3 = ((s8[6291456]{0:T(1024)(128)(4,1)}), s8[2097152]{0:T(1024)(128)(4,1)S(1)}, s32[]{:S(2)}) async-start(s8[6291456]{0:T(1024)(128)(4,1)} %bitcast.154), calls=%async_computation.3 | async-start | bytes 4194304
  207.5 9.1 %collective-permute-start.38 = (bf16[64,3072]{1,0:T(8,128)(2,1)S(1)}, bf16[64,3072]{1,0:T(8,128)(2,1)S(1)}, u32[]{:S(2)}, u32[]{:S(2)}) collective-permute-start(bf16[64,3072]{1,0:T(8,128)(2,1)S(1)} %fusion.25), channel_id=1, source_target_pairs={{0,8},{28,20},{8,16},{20,12},{16,24},{12,4},{1,9},{29,21},{9,17},{... | collective-permute-start | bytes 1179656 | tf_op jit(solution)/shard_map/ppermute | solution.py:117
  216.5 7.8 %collective-permute-start.39 = (bf16[64,3072]{1,0:T(8,128)(2,1)S(1)}, bf16[64,3072]{1,0:T(8,128)(2,1)S(1)}, u32[]{:S(2)}, u32[]{:S(2)}) collective-permute-start(bf16[64,3072]{1,0:T(8,128)(2,1)S(1)} %collective-permute-done.38), channel_id=1, source_target_pairs={{8,16},{20,12},{16,24},{12,4},{9,17},{21,13},{17,25},{13,5},{10,18... | collective-permute-start | bytes 1179656 | tf_op jit(solution)/shard_map/ppermute | solution.py:117
  217.2 12.4 %collective-permute-start.18 = (bf16[64,3072]{1,0:T(8,128)(2,1)S(1)}, bf16[64,3072]{1,0:T(8,128)(2,1)S(1)}, u32[]{:S(2)}, u32[]{:S(2)}) collective-permute-start(bf16[64,3072]{1,0:T(8,128)(2,1)S(1)} %fusion.33), channel_id=1, source_target_pairs={{0,8},{28,20},{8,16},{20,12},{16,24},{12,4},{1,9},{29,21},{9,17},{... | collective-permute-start | bytes 1179656 | tf_op jit(solution)/shard_map/ppermute | solution.py:117
  224.4 5.9 %collective-permute-start.40 = (bf16[64,3072]{1,0:T(8,128)(2,1)S(1)}, bf16[64,3072]{1,0:T(8,128)(2,1)S(1)}, u32[]{:S(2)}, u32[]{:S(2)}) collective-permute-start(bf16[64,3072]{1,0:T(8,128)(2,1)S(1)} %collective-permute-done.39), channel_id=1, source_target_pairs={{16,24},{12,4},{17,25},{13,5},{18,26},{14,6},{19,27},{15,7}} | collective-permute-start | bytes 1179656 | tf_op jit(solution)/shard_map/ppermute | solution.py:117
  229.6 4.4 %collective-permute-start.19 = (bf16[64,3072]{1,0:T(8,128)(2,1)S(1)}, bf16[64,3072]{1,0:T(8,128)(2,1)S(1)}, u32[]{:S(2)}, u32[]{:S(2)}) collective-permute-start(bf16[64,3072]{1,0:T(8,128)(2,1)S(1)} %collective-permute-done.18), channel_id=1, source_target_pairs={{8,16},{20,12},{16,24},{12,4},{9,17},{21,13},{17,25},{13,5},{10,18... | collective-permute-start | bytes 1179656 | tf_op jit(solution)/shard_map/ppermute | solution.py:117
  230.4 37.8 %collective-permute-start.41 = (bf16[3,64,3072]{2,1,0:T(8,128)(2,1)S(1)}, bf16[3,64,3072]{2,1,0:T(8,128)(2,1)S(1)}, u32[]{:S(2)}, u32[]{:S(2)}) collective-permute-start(bf16[3,64,3072]{2,1,0:T(8,128)(2,1)S(1)} %pad_maximum_fusion.7), channel_id=1, source_target_pairs={{0,4},{4,0},{1,5},{5,1},{2,6},{6,2},{3,7},{7,3},{8,12},{12,8},{9,1... | collective-permute-start | bytes 3538952 | tf_op jit(solution)/shard_map/ppermute | solution.py:109
  234.0 0.7 collective-permute-start.20
  234.9 34.2 %collective-permute-start.21 = (bf16[3,64,3072]{2,1,0:T(8,128)(2,1)S(1)}, bf16[3,64,3072]{2,1,0:T(8,128)(2,1)S(1)}, u32[]{:S(2)}, u32[]{:S(2)}) collective-permute-start(bf16[3,64,3072]{2,1,0:T(8,128)(2,1)S(1)} %pad_maximum_fusion.5), channel_id=1, source_target_pairs={{0,4},{4,0},{1,5},{5,1},{2,6},{6,2},{3,7},{7,3},{8,12},{12,8},{9,1... | collective-permute-start | bytes 3538952 | tf_op jit(solution)/shard_map/ppermute | solution.py:109
  261.5 9.0 %slice-start.10 = ((s8[6291456]{0:T(1024)(128)(4,1)}), s8[4194304]{0:T(1024)(128)(4,1)S(1)}, s32[]{:S(2)}) async-start(s8[6291456]{0:T(1024)(128)(4,1)} %bitcast.180), calls=%async_computation.10 | async-start | bytes 8388608
  264.9 5.6 %slice-start.11 = ((s8[6291456]{0:T(1024)(128)(4,1)}), s8[2097152]{0:T(1024)(128)(4,1)S(1)}, s32[]{:S(2)}) async-start(s8[6291456]{0:T(1024)(128)(4,1)} %bitcast.180), calls=%async_computation.11 | async-start | bytes 4194304
  268.6 2.2 slice-start.8
  269.1 2.6 slice-start.9
  271.6 2.8 copy-start.2
  274.4 13.2 %copy-start.1 = (bf16[256,1024]{1,0:T(8,128)(2,1)S(1)}, bf16[256,1024]{1,0:T(8,128)(2,1)}, u32[]{:S(2)}) copy-start(bf16[256,1024]{1,0:T(8,128)(2,1)} %param.9) | copy-start | bytes 1572868

commit v2 on v1

--- a/solution.py
+++ b/solution.py
@@ -11,7 +11,7 @@
 GROUPS = 2
 PIECES = 6
 LANES = 128
-VMEM_LIMIT = 24 * 2**20
+ENC_LIMIT = 36 * 2**20
 
 
 beta_one = 0.9
@@ -54,7 +54,7 @@
     second_out[...] = second_next.astype(bf16)
 
 
-def adam_rows(lefts, rights, weight, first, second, tile, scale=None, done=None, begin=0, end=None):
+def adam_rows(lefts, rights, weight, first, second, tile, limit, scale=None, done=None, begin=0, end=None):
     height, width = weight.shape
     end = height if end is None else end
     depth = lefts[0].shape[0]
@@ -92,7 +92,7 @@
             bytes_accessed=12 * part * width,
             transcendentals=2 * part * width,
         ),
-        compiler_params=pltpu.CompilerParams(vmem_limit_bytes=VMEM_LIMIT),
+        compiler_params=pltpu.CompilerParams(vmem_limit_bytes=limit),
         name="adam",
     )(*operands)
 
@@ -116,28 +116,37 @@
             pairs.append(((top - place) * 2 + 1, (top - place - 1) * 2 + 1))
         return lax.ppermute(value, ("z", "core"), pairs)
 
-    def flipped(self, blocks):
-        return jnp.concatenate([blocks[:1], blocks[1:][::-1]], axis=0)
-
-    def reduce_own(self, blocks, other, wire, earlier):
-        other = self.flipped(other)
+    def reduce_own(self, block, wire, earlier):
         carried = None
         for step in range(1, self.chips):
-            part = blocks[step].astype(f32) + other[step].astype(f32)
+            part = block(step)
             if carried is not None:
                 part = part + carried.astype(f32)
             carried = self.hop(part.astype(wire), 0, step - 1)
-        here = blocks[0].astype(f32) + other[0].astype(f32)
         away = after(self.sibling(carried), earlier)
-        return here + (carried.astype(f32) + away.astype(f32))
-
-    def gather_own(self, block):
-        got, carried = [], block
+        return block(0) + (carried.astype(f32) + away.astype(f32))
+
+    def gather_own(self, block, earlier):
+        got = [block]
         for step in range(1, self.chips):
-            carried = self.hop(carried, step - 1, self.chips - 2)
-            got.append(carried)
-        got = jnp.stack(got)
-        return jnp.concatenate([block[None], got + self.sibling(got)[::-1]], axis=0)
+            got.append(self.hop(got[-1], step - 1, self.chips - 2))
+        got[-1] = after(got[-1], earlier)
+        sent = jnp.stack([jnp.zeros_like(block), *got[:0:-1]])
+        away = self.sibling(sent)
+        return jnp.stack(got) + away, sent
+
+    def summed(self, parts, others, row_index):
+        sums = lambda t: [part[t].astype(f32) + other[-t].astype(f32) for part, other in zip(parts, others)]
+
+        def block(t):
+            found = sums(t)
+            if len(found) == 1:
+                return found[0]
+            own, away = found
+            here = row_index == 0
+            return jnp.concatenate([jnp.where(here, own, away), jnp.where(here, away, own)])
+
+        return block
 
     def partner(self, value, step):
         axes = [("row", 1)]
@@ -158,12 +167,14 @@
                     )
         return lax.ppermute(value, ("core", "latent", "row"), pairs)
 
-    def reduce_latents(self, part):
+    def reduce_latents(self, part, earlier):
         steps = 1 + (self.latents.bit_length() - 1)
         total = part
         for step in range(steps):
             sent = total.astype(bf16)
-            total = sent.astype(f32) + self.partner(sent, step).astype(f32)
+            got = self.partner(sent, step)
+            got = after(got, earlier if step == steps - 1 else None)
+            total = sent.astype(f32) + got.astype(f32)
         return total
 
 
@@ -194,12 +205,13 @@
     step_of = jnp.where(core == 0, -jnp.arange(chips), jnp.arange(chips))
     turned = jnp.take(turned, (place + step_of) % chips, axis=1)
 
-    tokens = []
+    tokens, halves = [], []
     for group in range(GROUPS):
         own = turned[group]
         away = after(lax.ppermute(own, "row", [(0, 1), (1, 0)]), tokens[-1] if tokens else None)
         first, second = jnp.where(row_index == 0, own, away), jnp.where(row_index == 0, away, own)
         tokens.append(jnp.concatenate([first, second], axis=1).reshape(chips * block_rows, shard_width))
+        halves.append((tokens[-1],))
 
     wide = dec_weight.astype(f32)
     partial_sq = jnp.sum(wide * wide, axis=1)
@@ -209,26 +221,32 @@
     penalty = sparsity * own_norm / (total_rows * shards_per_expert)
 
     lat, low, pre, col_total, row_bias, bias_sum = [], [], [], 0.0, 0.0, 0.0
-    first_block = second_block = grad_low = None
+    first_block = second_block = first_sent = second_sent = grad_low = None
     for group in range(GROUPS):
-        part = jnp.dot(tokens[group], enc_weight, preferred_element_type=f32)
-        part = part.reshape(chips, block_rows, local_latents)
-        preact = moves.reduce_own(part, moves.sibling(part), f32, first_block) + bias_here
+        parts, others = [], []
+        for rows in halves[group]:
+            rows = rows.reshape(-1, shard_width)
+            part = jnp.dot(rows, enc_weight, preferred_element_type=f32)
+            parts.append(part.reshape(chips, -1, local_latents))
+            others.append(moves.sibling(parts[-1]))
+        block = moves.summed(parts, others, row_index)
+        preact = moves.reduce_own(block, f32, first_block) + bias_here
         active = preact > 0
         first_block = jnp.maximum(preact, 0.0).astype(bf16)
-        latent = moves.gather_own(first_block)
+        latent, first_sent = moves.gather_own(first_block, first_sent)
         latent = latent.reshape(chips * block_rows, local_latents)
         rebuilt = jnp.dot(latent, dec_weight, preferred_element_type=f32)
-        rebuilt = after(moves.reduce_latents(rebuilt), grad_low)
+        rebuilt = moves.reduce_latents(rebuilt, grad_low)
         grad_rows = 2.0 * (rebuilt + dec_bias - tokens[group].astype(f32)) / total_rows
         grad_low = grad_rows.astype(bf16)
         back = lax.dot_general(
             grad_low, dec_weight, (((1,), (1,)), ((), ())), preferred_element_type=f32
         )
         back = (back + penalty).astype(bf16).reshape(chips, block_rows, local_latents)
-        back_grad = moves.reduce_own(back, moves.sibling(back), bf16, second_block)
+        block = moves.summed([back], [moves.sibling(back)], row_index)
+        back_grad = moves.reduce_own(block, bf16, second_block)
         second_block = jnp.where(active, back_grad, 0.0).astype(bf16)
-        grad_pre = moves.gather_own(second_block)
+        grad_pre, second_sent = moves.gather_own(second_block, second_sent)
         grad_pre = grad_pre.reshape(chips * block_rows, local_latents)
         lat.append(latent)
         low.append(grad_low)
@@ -245,11 +263,11 @@
     for piece in range(PIECES):
         begin = piece * piece_rows
         done = adam_rows(
-            lat, low, dec_weight, dec_first, dec_second, tile, scale, done, begin, begin + piece_rows
+            lat, low, dec_weight, dec_first, dec_second, tile, 24 * 2**20, scale, done, begin, begin + piece_rows
         )
     decoder_next, dec_first_next, dec_second_next = done
     encoder_next, enc_first_next, enc_second_next = adam_rows(
-        tokens, pre, enc_weight, enc_first, enc_second, LANES
+        tokens, pre, enc_weight, enc_first, enc_second, LANES, ENC_LIMIT
     )
     return (
         encoder_next,

time: 290 us -> 261 us (0.900)
  starting transfers between devices: 134 us -> 105 us
    ppermute x12, starting transfers between devices: 47.2 us -> 31.5 us  [sibling(): return lax.ppermute(value, 'core', [(0, 1), (1, 0)])]
    ppermute x24, starting transfers between devices: 78.1 us -> 65.5 us  [hop(): return lax.ppermute(value, ('z', 'core'), pairs)]
  transfers between devices with their start and end apart: 42 -> 42, of which waited for: 26 -> 24; matrix products, arithmetic and copies ran while one was open for 6% -> 7% of each run, Pallas kernels for 7% -> 8%
where the time goes in v2:
time: 261 us; the launch traced here: 260 us
  starting transfers between devices  105 us (40%)
  waiting for transfers between devices  85.9 us (33%)
  Pallas kernels  35.3 us (14%)
  matrix products  13.8 us (5%)
  other arithmetic  13.3 us (5%)
  local copies, waits for them, and re-layouts  4.93 us (2%)
    ppermute x24, starting transfers between devices, hop(): return lax.ppermute(value, ('z', 'core'), pairs)  65.5 us
    ppermute x24, waiting for transfers between devices, hop(): return lax.ppermute(value, ('z', 'core'), pairs)  48.2 us
    pallas_call x7, Pallas kernels, adam_rows(): pl.pallas_call(kernel, grid=(part // tile,), in_specs=in_specs, out_specs...  35.3 us
    ppermute x12, starting transfers between devices, sibling(): return lax.ppermute(value, 'core', [(0, 1), (1, 0)])  31.5 us
    ppermute x4, waiting for transfers between devices, partner(): return lax.ppermute(value, ('core', 'latent', 'row'), pairs)  18.1 us
    ppermute x2, waiting for transfers between devices, local(): lax.ppermute(own, 'row', [(0, 1), (1, 0)])  11.8 us
    ppermute x12, waiting for transfers between devices, sibling(): return lax.ppermute(value, 'core', [(0, 1), (1, 0)])  7.87 us
    dot_general x2, matrix products, local(): part = jnp.dot(rows, enc_weight, preferred_element_type=f32)  6.56 us
  transfers between devices with their start and end apart: 42, of which 24 were waited for; matrix products, arithmetic and copies ran while one was open for 7% of the time, Pallas kernels for 8%

profile of v2, /device:TPU:0, one launch (start us, length us, event | category | flops | bytes accessed | tf_op | source)
XLA Modules:
  0.0 260.1 jit_solution(3206077915705923078)
XLA Ops:
  0.7 1.0 copy-done
  2.4 3.0 %collective-permute-start = (bf16[4,32,1024]{2,1,0:T(8,128)(2,1)S(1)}, bf16[4,32,1024]{2,1,0:T(8,128)(2,1)S(1)}, u32[]{:S(2)}, u32[]{:S(2)}) collective-permute-start(bf16[4,32,1024]{2,1,0:T(8,128)(2,1)S(1)} %get-tuple-element.82), channel_id=1, source_target_pairs={{0,1},{1,0},{2,3},{3,2},{4,5},{5,4},{6,7},{7,6},{8,9},{9,8},{10,11... | collective-permute-start | bytes 786440 | tf_op jit(solution)/shard_map/ppermute | solution.py:211
  5.5 7.1 %collective-permute-done = bf16[4,32,1024]{2,1,0:T(8,128)(2,1)S(1)} collective-permute-done((bf16[4,32,1024]{2,1,0:T(8,128)(2,1)S(1)}, bf16[4,32,1024]{2,1,0:T(8,128)(2,1)S(1)}, u32[]{:S(2)}, u32[]{:S(2)}) %collective-permute-start) | collective-permute-done | bytes 262176 | tf_op jit(solution)/shard_map/ppermute | solution.py:211
  12.7 4.7 %collective-permute-done.1 = bf16[4,32,1024]{2,1,0:T(8,128)(2,1)S(1)} collective-permute-done((bf16[4,32,1024]{2,1,0:T(8,128)(2,1)S(1)}, bf16[4,32,1024]{2,1,0:T(8,128)(2,1)S(1)}, u32[]{:S(2)}, u32[]{:S(2)}) %collective-permute-start.1) | collective-permute-done | bytes 262176 | tf_op jit(solution)/shard_map/ppermute | solution.py:211
  17.4 4.7 %fusion.62 = f32[256,3072]{1,0:T(8,128)S(1)} fusion(bf16[256,1024]{1,0:T(8,128)(2,1)S(1)} %bitcast.173, bf16[1024,3072]{1,0:T(8,128)(2,1)} %refs_4_.7), kind=kOutput, calls=%fused_computation.127 | convolution fusion | flops 1610612736 | bytes 9961472 | tf_op jit(solution)/shard_map/dot_general | solution.py:229
  22.3 1.8 fusion.63
  24.7 3.1 %collective-permute-done.2 = f32[4,64,3072]{2,1,0:T(8,128)S(1)} collective-permute-done((f32[4,64,3072]{2,1,0:T(8,128)S(1)}, f32[4,64,3072]{2,1,0:T(8,128)S(1)}, u32[]{:S(2)}, u32[]{:S(2)}) %collective-permute-start.2) | collective-permute-done | bytes 3145760 | tf_op jit(solution)/shard_map/ppermute | solution.py:109
  28.0 3.8 %collective-permute-start.3 = (f32[64,3072]{1,0:T(8,128)S(1)}, f32[64,3072]{1,0:T(8,128)S(1)}, u32[]{:S(2)}, u32[]{:S(2)}) collective-permute-start(f32[64,3072]{1,0:T(8,128)S(1)} %fusion.22), channel_id=1, source_target_pairs={{0,8},{28,20},{1,9},{29,21},{2,10},{30,22},{3,11},{31,23}} | collective-permute-start | bytes 2359304 | tf_op jit(solution)/shard_map/ppermute | solution.py:117
  32.5 3.8 %collective-permute-start.23 = (f32[64,3072]{1,0:T(8,128)S(1)}, f32[64,3072]{1,0:T(8,128)S(1)}, u32[]{:S(2)}, u32[]{:S(2)}) collective-permute-start(f32[64,3072]{1,0:T(8,128)S(1)} %fusion.14), channel_id=1, source_target_pairs={{0,8},{28,20},{1,9},{29,21},{2,10},{30,22},{3,11},{31,23}} | collective-permute-start | bytes 2359304 | tf_op jit(solution)/shard_map/ppermute | solution.py:117
  36.3 4.9 %collective-permute-done.3 = f32[64,3072]{1,0:T(8,128)S(1)} collective-permute-done((f32[64,3072]{1,0:T(8,128)S(1)}, f32[64,3072]{1,0:T(8,128)S(1)}, u32[]{:S(2)}, u32[]{:S(2)}) %collective-permute-start.3) | collective-permute-done | bytes 786464 | tf_op jit(solution)/shard_map/ppermute | solution.py:117
  41.3 4.4 %collective-permute-start.4 = (f32[64,3072]{1,0:T(8,128)S(1)}, f32[64,3072]{1,0:T(8,128)S(1)}, u32[]{:S(2)}, u32[]{:S(2)}) collective-permute-start(f32[64,3072]{1,0:T(8,128)S(1)} %fusion.24), channel_id=1, source_target_pairs={{0,8},{28,20},{8,16},{20,12},{1,9},{29,21},{9,17},{21,13},{2,10},{... | collective-permute-start | bytes 2359304 | tf_op jit(solution)/shard_map/ppermute | solution.py:117
  45.8 3.8 %collective-permute-done.23 = f32[64,3072]{1,0:T(8,128)S(1)} collective-permute-done((f32[64,3072]{1,0:T(8,128)S(1)}, f32[64,3072]{1,0:T(8,128)S(1)}, u32[]{:S(2)}, u32[]{:S(2)}) %collective-permute-start.23) | collective-permute-done | bytes 786464 | tf_op jit(solution)/shard_map/ppermute | solution.py:117
  49.8 4.4 %collective-permute-start.24 = (f32[64,3072]{1,0:T(8,128)S(1)}, f32[64,3072]{1,0:T(8,128)S(1)}, u32[]{:S(2)}, u32[]{:S(2)}) collective-permute-start(f32[64,3072]{1,0:T(8,128)S(1)} %fusion.16), channel_id=1, source_target_pairs={{0,8},{28,20},{8,16},{20,12},{1,9},{29,21},{9,17},{21,13},{2,10},{... | collective-permute-start | bytes 2359304 | tf_op jit(solution)/shard_map/ppermute | solution.py:117
  54.2 3.8 %collective-permute-done.4 = f32[64,3072]{1,0:T(8,128)S(1)} collective-permute-done((f32[64,3072]{1,0:T(8,128)S(1)}, f32[64,3072]{1,0:T(8,128)S(1)}, u32[]{:S(2)}, u32[]{:S(2)}) %collective-permute-start.4) | collective-permute-done | bytes 786464 | tf_op jit(solution)/shard_map/ppermute | solution.py:117
  58.2 4.4 %collective-permute-start.5 = (f32[64,3072]{1,0:T(8,128)S(1)}, f32[64,3072]{1,0:T(8,128)S(1)}, u32[]{:S(2)}, u32[]{:S(2)}) collective-permute-start(f32[64,3072]{1,0:T(8,128)S(1)} %fusion.26), channel_id=1, source_target_pairs={{0,8},{28,20},{8,16},{20,12},{16,24},{12,4},{1,9},{29,21},{9,17},{... | collective-permute-start | bytes 2359304 | tf_op jit(solution)/shard_map/ppermute | solution.py:117
  62.7 3.8 %collective-permute-done.24 = f32[64,3072]{1,0:T(8,128)S(1)} collective-permute-done((f32[64,3072]{1,0:T(8,128)S(1)}, f32[64,3072]{1,0:T(8,128)S(1)}, u32[]{:S(2)}, u32[]{:S(2)}) %collective-permute-start.24) | collective-permute-done | bytes 786464 | tf_op jit(solution)/shard_map/ppermute | solution.py:117
  66.6 4.4 %collective-permute-start.25 = (f32[64,3072]{1,0:T(8,128)S(1)}, f32[64,3072]{1,0:T(8,128)S(1)}, u32[]{:S(2)}, u32[]{:S(2)}) collective-permute-start(f32[64,3072]{1,0:T(8,128)S(1)} %fusion.18), channel_id=1, source_target_pairs={{0,8},{28,20},{8,16},{20,12},{16,24},{12,4},{1,9},{29,21},{9,17},{... | collective-permute-start | bytes 2359304 | tf_op jit(solution)/shard_map/ppermute | solution.py:117
  71.1 3.8 %collective-permute-done.5 = f32[64,3072]{1,0:T(8,128)S(1)} collective-permute-done((f32[64,3072]{1,0:T(8,128)S(1)}, f32[64,3072]{1,0:T(8,128)S(1)}, u32[]{:S(2)}, u32[]{:S(2)}) %collective-permute-start.5) | collective-permute-done | bytes 786464 | tf_op jit(solution)/shard_map/ppermute | solution.py:117
  74.9 8.4 %collective-permute-done.25 = f32[64,3072]{1,0:T(8,128)S(1)} collective-permute-done((f32[64,3072]{1,0:T(8,128)S(1)}, f32[64,3072]{1,0:T(8,128)S(1)}, u32[]{:S(2)}, u32[]{:S(2)}) %collective-permute-start.25) | collective-permute-done | bytes 786464 | tf_op jit(solution)/shard_map/ppermute | solution.py:117
  83.3 1.9 maximum_convert_fusion.1
  85.3 4.5 %collective-permute-start.7 = (bf16[64,3072]{1,0:T(8,128)(2,1)S(1)}, bf16[64,3072]{1,0:T(8,128)(2,1)S(1)}, u32[]{:S(2)}, u32[]{:S(2)}) collective-permute-start(bf16[64,3072]{1,0:T(8,128)(2,1)S(1)} %get-tuple-element.74), channel_id=1, source_target_pairs={{0,8},{28,20},{8,16},{20,12},{16,24},{12,4},{1,9},{29,21},{9,17},{... | collective-permute-start | bytes 1179656 | tf_op jit(solution)/shard_map/ppermute | solution.py:117
  89.9 1.8 maximum_convert_fusion
  91.6 2.5 collective-permute-start.27
  94.1 1.0 collective-permute-done.7
  95.8 3.6 %collective-permute-done.27 = bf16[64,3072]{1,0:T(8,128)(2,1)S(1)} collective-permute-done((bf16[64,3072]{1,0:T(8,128)(2,1)S(1)}, bf16[64,3072]{1,0:T(8,128)(2,1)S(1)}, u32[]{:S(2)}, u32[]{:S(2)}) %collective-permute-start.27) | collective-permute-done | bytes 393248 | tf_op jit(solution)/shard_map/ppermute | solution.py:117
  100.8 0.9 collective-permute-start.29
  102.1 14.9 %collective-permute-start.30 = (bf16[4,64,3072]{2,1,0:T(8,128)(2,1)S(1)}, bf16[4,64,3072]{2,1,0:T(8,128)(2,1)S(1)}, u32[]{:S(2)}, u32[]{:S(2)}) collective-permute-start(bf16[4,64,3072]{2,1,0:T(8,128)(2,1)S(1)} %fusion.7), channel_id=1, source_target_pairs={{0,4},{4,0},{1,5},{5,1},{2,6},{6,2},{3,7},{7,3},{8,12},{12,8},{9,1... | collective-permute-start | bytes 4718600 | tf_op jit(solution)/shard_map/ppermute | solution.py:109
  117.1 3.0 %collective-permute-done.30 = bf16[4,64,3072]{2,1,0:T(8,128)(2,1)S(1)} collective-permute-done((bf16[4,64,3072]{2,1,0:T(8,128)(2,1)S(1)}, bf16[4,64,3072]{2,1,0:T(8,128)(2,1)S(1)}, u32[]{:S(2)}, u32[]{:S(2)}) %collective-permute-start.30) | collective-permute-done | bytes 1572896 | tf_op jit(solution)/shard_map/ppermute | solution.py:109
  120.7 1.8 convolution_convert_fusion
  122.5 1.6 collective-permute-start.31
  124.6 1.8 convolution_convert_fusion.1
  127.0 4.7 %collective-permute-done.31 = bf16[256,1024]{1,0:T(8,128)(2,1)S(1)} collective-permute-done((bf16[256,1024]{1,0:T(8,128)(2,1)S(1)}, bf16[256,1024]{1,0:T(8,128)(2,1)S(1)}, u32[]{:S(2)}, u32[]{:S(2)}) %collective-permute-start.31) | collective-permute-done | bytes 524320 | tf_op jit(solution)/shard_map/ppermute | solution.py:168
  131.9 1.6 collective-permute-start.32
  133.5 7.1 %collective-permute-done.11 = bf16[256,1024]{1,0:T(8,128)(2,1)S(1)} collective-permute-done((bf16[256,1024]{1,0:T(8,128)(2,1)S(1)}, bf16[256,1024]{1,0:T(8,128)(2,1)S(1)}, u32[]{:S(2)}, u32[]{:S(2)}) %collective-permute-start.11) | collective-permute-done | bytes 524320 | tf_op jit(solution)/shard_map/ppermute | solution.py:168
  140.8 1.6 collective-permute-start.12
  142.4 1.3 multiply_reduce_fusion
  143.7 6.3 %collective-permute-done.12 = bf16[256,1024]{1,0:T(8,128)(2,1)S(1)} collective-permute-done((bf16[256,1024]{1,0:T(8,128)(2,1)S(1)}, bf16[256,1024]{1,0:T(8,128)(2,1)S(1)}, u32[]{:S(2)}, u32[]{:S(2)}) %collective-permute-start.12) | collective-permute-done | bytes 524320 | tf_op jit(solution)/shard_map/ppermute | solution.py:168
  150.4 1.8 fusion
  152.3 0.8 fusion.48
  153.1 1.8 fusion.1
  155.8 1.8 collective-permute-start.14
  157.5 0.9 collective-permute-done.33
  158.6 1.8 collective-permute-start.34
  160.4 2.4 collective-permute-done.14
  162.9 4.7 %collective-permute-start.15 = (bf16[64,3072]{1,0:T(8,128)(2,1)S(1)}, bf16[64,3072]{1,0:T(8,128)(2,1)S(1)}, u32[]{:S(2)}, u32[]{:S(2)}) collective-permute-start(bf16[64,3072]{1,0:T(8,128)(2,1)S(1)} %fusion.40), channel_id=1, source_target_pairs={{0,8},{28,20},{8,16},{20,12},{1,9},{29,21},{9,17},{21,13},{2,10},{... | collective-permute-start | bytes 1179656 | tf_op jit(solution)/shard_map/ppermute | solution.py:117
  167.8 4.0 %collective-permute-start.35 = (bf16[64,3072]{1,0:T(8,128)(2,1)S(1)}, bf16[64,3072]{1,0:T(8,128)(2,1)S(1)}, u32[]{:S(2)}, u32[]{:S(2)}) collective-permute-start(bf16[64,3072]{1,0:T(8,128)(2,1)S(1)} %fusion.32), channel_id=1, source_target_pairs={{0,8},{28,20},{8,16},{20,12},{1,9},{29,21},{9,17},{21,13},{2,10},{... | collective-permute-start | bytes 1179656 | tf_op jit(solution)/shard_map/ppermute | solution.py:117
  171.8 1.1 collective-permute-done.15
  173.0 4.7 %collective-permute-start.16 = (bf16[64,3072]{1,0:T(8,128)(2,1)S(1)}, bf16[64,3072]{1,0:T(8,128)(2,1)S(1)}, u32[]{:S(2)}, u32[]{:S(2)}) collective-permute-start(bf16[64,3072]{1,0:T(8,128)(2,1)S(1)} %fusion.42), channel_id=1, source_target_pairs={{0,8},{28,20},{8,16},{20,12},{16,24},{12,4},{1,9},{29,21},{9,17},{... | collective-permute-start | bytes 1179656 | tf_op jit(solution)/shard_map/ppermute | solution.py:117
  177.9 3.8 %collective-permute-start.36 = (bf16[64,3072]{1,0:T(8,128)(2,1)S(1)}, bf16[64,3072]{1,0:T(8,128)(2,1)S(1)}, u32[]{:S(2)}, u32[]{:S(2)}) collective-permute-start(bf16[64,3072]{1,0:T(8,128)(2,1)S(1)} %fusion.34), channel_id=1, source_target_pairs={{0,8},{28,20},{8,16},{20,12},{16,24},{12,4},{1,9},{29,21},{9,17},{... | collective-permute-start | bytes 1179656 | tf_op jit(solution)/shard_map/ppermute | solution.py:117
  181.7 1.3 collective-permute-done.16
  183.0 4.2 %collective-permute-done.36 = bf16[64,3072]{1,0:T(8,128)(2,1)S(1)} collective-permute-done((bf16[64,3072]{1,0:T(8,128)(2,1)S(1)}, bf16[64,3072]{1,0:T(8,128)(2,1)S(1)}, u32[]{:S(2)}, u32[]{:S(2)}) %collective-permute-start.36) | collective-permute-done | bytes 393248 | tf_op jit(solution)/shard_map/ppermute | solution.py:117
  187.4 4.4 %collective-permute-start.18 = (bf16[64,3072]{1,0:T(8,128)(2,1)S(1)}, bf16[64,3072]{1,0:T(8,128)(2,1)S(1)}, u32[]{:S(2)}, u32[]{:S(2)}) collective-permute-start(bf16[64,3072]{1,0:T(8,128)(2,1)S(1)} %fusion.45), channel_id=1, source_target_pairs={{0,8},{28,20},{8,16},{20,12},{16,24},{12,4},{1,9},{29,21},{9,17},{... | collective-permute-start | bytes 1179656 | tf_op jit(solution)/shard_map/ppermute | solution.py:117
  192.2 2.5 collective-permute-start.38
  194.7 2.4 collective-permute-done.18
  197.8 3.5 %collective-permute-done.38 = bf16[64,3072]{1,0:T(8,128)(2,1)S(1)} collective-permute-done((bf16[64,3072]{1,0:T(8,128)(2,1)S(1)}, bf16[64,3072]{1,0:T(8,128)(2,1)S(1)}, u32[]{:S(2)}, u32[]{:S(2)}) %collective-permute-start.38) | collective-permute-done | bytes 393248 | tf_op jit(solution)/shard_map/ppermute | solution.py:117
  203.8 15.2 %collective-permute-start.41 = (bf16[4,64,3072]{2,1,0:T(8,128)(2,1)S(1)}, bf16[4,64,3072]{2,1,0:T(8,128)(2,1)S(1)}, u32[]{:S(2)}, u32[]{:S(2)}) collective-permute-start(bf16[4,64,3072]{2,1,0:T(8,128)(2,1)S(1)} %fusion.4), channel_id=1, source_target_pairs={{0,4},{4,0},{1,5},{5,1},{2,6},{6,2},{3,7},{7,3},{8,12},{12,8},{9,1... | collective-permute-start | bytes 4718600 | tf_op jit(solution)/shard_map/ppermute | solution.py:109
  220.2 3.4 %adam.8 = (bf16[3072,1024]{1,0:T(8,128)(2,1)}, bf16[3072,1024]{1,0:T(8,128)(2,1)}, bf16[3072,1024]{1,0:T(8,128)(2,1)}) custom-call(bf16[256,3072]{1,0:T(8,128)(2,1)S(1)} %bitcast.167, bf16[256,3072]{1,0:T(8,128)(2,1)S(1)} %bitcast.160, bf16[256,1024]{1,0:T(8,128)(2,1)S(1)} %fusion.47.refs_2_, bf16[256,1024]{1,0:T(8,128)(2,1)S(1)} %get-tuple-element.76.refs_3_, ...), custom_call_target="tpu_custom_call" | custom-call | flops 536870912 | bytes 6291456 | tf_op jit(solution)/shard_map/adam/pallas_call | solution.py:82
  223.6 3.3 %adam.9 = (bf16[3072,1024]{1,0:T(8,128)(2,1)}, bf16[3072,1024]{1,0:T(8,128)(2,1)}, bf16[3072,1024]{1,0:T(8,128)(2,1)}) custom-call(bf16[256,3072]{1,0:T(8,128)(2,1)S(1)} %bitcast.168, bf16[256,3072]{1,0:T(8,128)(2,1)S(1)} %bitcast.161, bf16[256,1024]{1,0:T(8,128)(2,1)S(1)} %fusion.47.refs_2_, ...), custom_call_target="tpu_custom_call", output_to_operand_aliasing={{0}: (8, {}), {1}: (9, {}), {2}: (10, {})} | custom-call | flops 536870912 | bytes 6291456 | tf_op jit(solution)/shard_map/adam/pallas_call | solution.py:82
  226.9 3.3 %adam.10 = (bf16[3072,1024]{1,0:T(8,128)(2,1)}, bf16[3072,1024]{1,0:T(8,128)(2,1)}, bf16[3072,1024]{1,0:T(8,128)(2,1)}) custom-call(bf16[256,3072]{1,0:T(8,128)(2,1)S(1)} %bitcast.169, bf16[256,3072]{1,0:T(8,128)(2,1)S(1)} %bitcast.162, bf16[256,1024]{1,0:T(8,128)(2,1)S(1)} %fusion.47.refs_2_, ...), custom_call_target="tpu_custom_call", output_to_operand_aliasing={{0}: (8, {}), {1}: (9, {}), {2}: (10, {})} | custom-call | flops 536870912 | bytes 6291456 | tf_op jit(solution)/shard_map/adam/pallas_call | solution.py:82
  230.2 3.3 %adam.11 = (bf16[3072,1024]{1,0:T(8,128)(2,1)}, bf16[3072,1024]{1,0:T(8,128)(2,1)}, bf16[3072,1024]{1,0:T(8,128)(2,1)}) custom-call(bf16[256,3072]{1,0:T(8,128)(2,1)S(1)} %bitcast.170, bf16[256,3072]{1,0:T(8,128)(2,1)S(1)} %bitcast.163, bf16[256,1024]{1,0:T(8,128)(2,1)S(1)} %fusion.47.refs_2_, ...), custom_call_target="tpu_custom_call", output_to_operand_aliasing={{0}: (8, {}), {1}: (9, {}), {2}: (10, {})} | custom-call | flops 536870912 | bytes 6291456 | tf_op jit(solution)/shard_map/adam/pallas_call | solution.py:82
  233.6 3.3 %adam.12 = (bf16[3072,1024]{1,0:T(8,128)(2,1)}, bf16[3072,1024]{1,0:T(8,128)(2,1)}, bf16[3072,1024]{1,0:T(8,128)(2,1)}) custom-call(bf16[256,3072]{1,0:T(8,128)(2,1)S(1)} %bitcast.171, bf16[256,3072]{1,0:T(8,128)(2,1)S(1)} %bitcast.164, bf16[256,1024]{1,0:T(8,128)(2,1)S(1)} %fusion.47.refs_2_, ...), custom_call_target="tpu_custom_call", output_to_operand_aliasing={{0}: (8, {}), {1}: (9, {}), {2}: (10, {})} | custom-call | flops 536870912 | bytes 6291456 | tf_op jit(solution)/shard_map/adam/pallas_call | solution.py:82
  236.9 3.4 %adam.13 = (bf16[3072,1024]{1,0:T(8,128)(2,1)}, bf16[3072,1024]{1,0:T(8,128)(2,1)}, bf16[3072,1024]{1,0:T(8,128)(2,1)}) custom-call(bf16[256,3072]{1,0:T(8,128)(2,1)S(1)} %bitcast.172, bf16[256,3072]{1,0:T(8,128)(2,1)S(1)} %bitcast.165, bf16[256,1024]{1,0:T(8,128)(2,1)S(1)} %fusion.47.refs_2_, ...), custom_call_target="tpu_custom_call", output_to_operand_aliasing={{0}: (8, {}), {1}: (9, {}), {2}: (10, {})} | custom-call | flops 536870912 | bytes 6291456 | tf_op jit(solution)/shard_map/adam/pallas_call | solution.py:82
  242.1 2.8 %copy-done.2 = bf16[1024,3072]{1,0:T(8,128)(2,1)S(1)} copy-done((bf16[1024,3072]{1,0:T(8,128)(2,1)S(1)}, bf16[1024,3072]{1,0:T(8,128)(2,1)}, u32[]{:S(2)}) %copy-start.2) | copy-done | bytes 6291480
  244.9 15.2 %adam.7 = (bf16[1024,3072]{1,0:T(8,128)(2,1)}, bf16[1024,3072]{1,0:T(8,128)(2,1)}, bf16[1024,3072]{1,0:T(8,128)(2,1)}) custom-call(bf16[256,1024]{1,0:T(8,128)(2,1)S(1)} %bitcast.174, bf16[256,1024]{1,0:T(8,128)(2,1)S(1)} %bitcast.182, bf16[256,3072]{1,0:T(8,128)(2,1)S(1)} %bitcast.176, bf16[256,3072]{1,0:T(8,128)(2,1)S(1)} %bitcast.175, ...), custom_call_target="tpu_custom_call" | custom-call | flops 3221225472 | bytes 37748736 | tf_op jit(solution)/shard_map/adam/pallas_call | solution.py:82
  (121 shorter events, 16.5 us)
Async XLA Ops:
  0.6 1.1 copy-start
  2.4 10.2 %collective-permute-start = (bf16[4,32,1024]{2,1,0:T(8,128)(2,1)S(1)}, bf16[4,32,1024]{2,1,0:T(8,128)(2,1)S(1)}, u32[]{:S(2)}, u32[]{:S(2)}) collective-permute-start(bf16[4,32,1024]{2,1,0:T(8,128)(2,1)S(1)} %get-tuple-element.82), channel_id=1, source_target_pairs={{0,1},{1,0},{2,3},{3,2},{4,5},{5,4},{6,7},{7,6},{8,9},{9,8},{10,11... | collective-permute-start | bytes 786440 | tf_op jit(solution)/shard_map/ppermute | solution.py:211
  5.5 11.9 %collective-permute-start.1 = (bf16[4,32,1024]{2,1,0:T(8,128)(2,1)S(1)}, bf16[4,32,1024]{2,1,0:T(8,128)(2,1)S(1)}, u32[]{:S(2)}, u32[]{:S(2)}) collective-permute-start(bf16[4,32,1024]{2,1,0:T(8,128)(2,1)S(1)} %get-tuple-element.81), channel_id=1, source_target_pairs={{0,1},{1,0},{2,3},{3,2},{4,5},{5,4},{6,7},{7,6},{8,9},{9,8},{10,11... | collective-permute-start | bytes 786440 | tf_op jit(solution)/shard_map/ppermute | solution.py:211
  17.4 4.9 %slice-start.6 = ((s8[6291456]{0:T(1024)(128)(4,1)}), s8[4194304]{0:T(1024)(128)(4,1)S(1)}, s32[]{:S(2)}) async-start(s8[6291456]{0:T(1024)(128)(4,1)} %bitcast.177), calls=%async_computation.6 | async-start | bytes 8388608
  17.4 4.9 %slice-start.7 = ((s8[6291456]{0:T(1024)(128)(4,1)}), s8[2097152]{0:T(1024)(128)(4,1)S(1)}, s32[]{:S(2)}) async-start(s8[6291456]{0:T(1024)(128)(4,1)} %bitcast.177), calls=%async_computation.7 | async-start | bytes 4194304
  22.1 35.9 %copy-start.3 = (f32[256,3072]{1,0:T(8,128)}, f32[256,3072]{1,0:T(8,128)S(1)}, u32[]{:S(2)}) copy-start(f32[256,3072]{1,0:T(8,128)S(1)} %fusion.62) | copy-start | bytes 9437188
  22.1 5.7 %collective-permute-start.2 = (f32[4,64,3072]{2,1,0:T(8,128)S(1)}, f32[4,64,3072]{2,1,0:T(8,128)S(1)}, u32[]{:S(2)}, u32[]{:S(2)}) collective-permute-start(f32[4,64,3072]{2,1,0:T(8,128)S(1)} %bitcast.183), channel_id=1, source_target_pairs={{0,4},{4,0},{1,5},{5,1},{2,6},{6,2},{3,7},{7,3},{8,12},{12,8},{9,1... | collective-permute-start | bytes 9437192 | tf_op jit(solution)/shard_map/ppermute | solution.py:109
  24.2 42.3 %copy-start.4 = (f32[256,3072]{1,0:T(8,128)}, f32[256,3072]{1,0:T(8,128)S(1)}, u32[]{:S(2)}) copy-start(f32[256,3072]{1,0:T(8,128)S(1)} %fusion.63) | copy-start | bytes 9437188
  24.2 8.2 %collective-permute-start.22 = (f32[4,64,3072]{2,1,0:T(8,128)S(1)}, f32[4,64,3072]{2,1,0:T(8,128)S(1)}, u32[]{:S(2)}, u32[]{:S(2)}) collective-permute-start(f32[4,64,3072]{2,1,0:T(8,128)S(1)} %bitcast.184), channel_id=1, source_target_pairs={{0,4},{4,0},{1,5},{5,1},{2,6},{6,2},{3,7},{7,3},{8,12},{12,8},{9,1... | collective-permute-start | bytes 9437192 | tf_op jit(solution)/shard_map/ppermute | solution.py:109
  27.9 30.2 %copy-start.5 = (f32[4,64,3072]{2,1,0:T(8,128)}, f32[4,64,3072]{2,1,0:T(8,128)S(1)}, u32[]{:S(2)}) copy-start(f32[4,64,3072]{2,1,0:T(8,128)S(1)} %collective-permute-done.2) | copy-start | bytes 9437188
  28.0 13.2 %collective-permute-start.3 = (f32[64,3072]{1,0:T(8,128)S(1)}, f32[64,3072]{1,0:T(8,128)S(1)}, u32[]{:S(2)}, u32[]{:S(2)}) collective-permute-start(f32[64,3072]{1,0:T(8,128)S(1)} %fusion.22), channel_id=1, source_target_pairs={{0,8},{28,20},{1,9},{29,21},{2,10},{30,22},{3,11},{31,23}} | collective-permute-start | bytes 2359304 | tf_op jit(solution)/shard_map/ppermute | solution.py:117
  32.4 34.1 %copy-start.6 = (f32[4,64,3072]{2,1,0:T(8,128)}, f32[4,64,3072]{2,1,0:T(8,128)S(1)}, u32[]{:S(2)}) copy-start(f32[4,64,3072]{2,1,0:T(8,128)S(1)} %collective-permute-done.22) | copy-start | bytes 9437188
  32.5 17.1 %collective-permute-start.23 = (f32[64,3072]{1,0:T(8,128)S(1)}, f32[64,3072]{1,0:T(8,128)S(1)}, u32[]{:S(2)}, u32[]{:S(2)}) collective-permute-start(f32[64,3072]{1,0:T(8,128)S(1)} %fusion.14), channel_id=1, source_target_pairs={{0,8},{28,20},{1,9},{29,21},{2,10},{30,22},{3,11},{31,23}} | collective-permute-start | bytes 2359304 | tf_op jit(solution)/shard_map/ppermute | solution.py:117
  41.3 16.7 %collective-permute-start.4 = (f32[64,3072]{1,0:T(8,128)S(1)}, f32[64,3072]{1,0:T(8,128)S(1)}, u32[]{:S(2)}, u32[]{:S(2)}) collective-permute-start(f32[64,3072]{1,0:T(8,128)S(1)} %fusion.24), channel_id=1, source_target_pairs={{0,8},{28,20},{8,16},{20,12},{1,9},{29,21},{9,17},{21,13},{2,10},{... | collective-permute-start | bytes 2359304 | tf_op jit(solution)/shard_map/ppermute | solution.py:117
  49.8 16.7 %collective-permute-start.24 = (f32[64,3072]{1,0:T(8,128)S(1)}, f32[64,3072]{1,0:T(8,128)S(1)}, u32[]{:S(2)}, u32[]{:S(2)}) collective-permute-start(f32[64,3072]{1,0:T(8,128)S(1)} %fusion.16), channel_id=1, source_target_pairs={{0,8},{28,20},{8,16},{20,12},{1,9},{29,21},{9,17},{21,13},{2,10},{... | collective-permute-start | bytes 2359304 | tf_op jit(solution)/shard_map/ppermute | solution.py:117
  58.2 25.1 %copy-start.8 = (f32[6144]{0:T(1024)S(1)}, f32[6144]{0:T(1024)}, u32[]{:S(2)}) copy-start(f32[6144]{0:T(1024)} %param.12) | copy-start | bytes 73732
  58.2 16.7 %collective-permute-start.5 = (f32[64,3072]{1,0:T(8,128)S(1)}, f32[64,3072]{1,0:T(8,128)S(1)}, u32[]{:S(2)}, u32[]{:S(2)}) collective-permute-start(f32[64,3072]{1,0:T(8,128)S(1)} %fusion.26), channel_id=1, source_target_pairs={{0,8},{28,20},{8,16},{20,12},{16,24},{12,4},{1,9},{29,21},{9,17},{... | collective-permute-start | bytes 2359304 | tf_op jit(solution)/shard_map/ppermute | solution.py:117
  66.6 16.7 %collective-permute-start.25 = (f32[64,3072]{1,0:T(8,128)S(1)}, f32[64,3072]{1,0:T(8,128)S(1)}, u32[]{:S(2)}, u32[]{:S(2)}) collective-permute-start(f32[64,3072]{1,0:T(8,128)S(1)} %fusion.18), channel_id=1, source_target_pairs={{0,8},{28,20},{8,16},{20,12},{16,24},{12,4},{1,9},{29,21},{9,17},{... | collective-permute-start | bytes 2359304 | tf_op jit(solution)/shard_map/ppermute | solution.py:117
  74.9 8.4 %collective-permute-start.6 = (f32[64,3072]{1,0:T(8,128)S(1)}, f32[64,3072]{1,0:T(8,128)}, u32[]{:S(2)}, u32[]{:S(2)}) collective-permute-start(f32[64,3072]{1,0:T(8,128)S(1)} %collective-permute-done.5), channel_id=1, source_target_pairs={{0,4},{4,0},{1,5},{5,1},{2,6},{6,2},{3,7},{7,3},{8,12},{12,8},{9,1... | collective-permute-start | bytes 2359304 | tf_op jit(solution)/shard_map/ppermute | solution.py:109
  83.3 6.5 %collective-permute-start.26 = (f32[64,3072]{1,0:T(8,128)S(1)}, f32[64,3072]{1,0:T(8,128)}, u32[]{:S(2)}, u32[]{:S(2)}) collective-permute-start(f32[64,3072]{1,0:T(8,128)S(1)} %collective-permute-done.25), channel_id=1, source_target_pairs={{0,4},{4,0},{1,5},{5,1},{2,6},{6,2},{3,7},{7,3},{8,12},{12,8},{9,1... | collective-permute-start | bytes 2359304 | tf_op jit(solution)/shard_map/ppermute | solution.py:109
  83.3 37.3 %slice-start = ((s8[6291456]{0:T(1024)(128)(4,1)}), s8[4194304]{0:T(1024)(128)(4,1)S(1)}, s32[]{:S(2)}) async-start(s8[6291456]{0:T(1024)(128)(4,1)} %bitcast.153), calls=%async_computation | async-start | bytes 8388608
  85.3 9.8 %collective-permute-start.7 = (bf16[64,3072]{1,0:T(8,128)(2,1)S(1)}, bf16[64,3072]{1,0:T(8,128)(2,1)S(1)}, u32[]{:S(2)}, u32[]{:S(2)}) collective-permute-start(bf16[64,3072]{1,0:T(8,128)(2,1)S(1)} %get-tuple-element.74), channel_id=1, source_target_pairs={{0,8},{28,20},{8,16},{20,12},{16,24},{12,4},{1,9},{29,21},{9,17},{... | collective-permute-start | bytes 1179656 | tf_op jit(solution)/shard_map/ppermute | solution.py:117
  91.6 7.7 %collective-permute-start.27 = (bf16[64,3072]{1,0:T(8,128)(2,1)S(1)}, bf16[64,3072]{1,0:T(8,128)(2,1)S(1)}, u32[]{:S(2)}, u32[]{:S(2)}) collective-permute-start(bf16[64,3072]{1,0:T(8,128)(2,1)S(1)} %get-tuple-element.72), channel_id=1, source_target_pairs={{0,8},{28,20},{8,16},{20,12},{16,24},{12,4},{1,9},{29,21},{9,17},{... | collective-permute-start | bytes 1179656 | tf_op jit(solution)/shard_map/ppermute | solution.py:117
  95.1 5.0 %collective-permute-start.8 = (bf16[64,3072]{1,0:T(8,128)(2,1)S(1)}, bf16[64,3072]{1,0:T(8,128)(2,1)S(1)}, u32[]{:S(2)}, u32[]{:S(2)}) collective-permute-start(bf16[64,3072]{1,0:T(8,128)(2,1)S(1)} %collective-permute-done.7), channel_id=1, source_target_pairs={{8,16},{20,12},{16,24},{12,4},{9,17},{21,13},{17,25},{13,5},{10,18... | collective-permute-start | bytes 1179656 | tf_op jit(solution)/shard_map/ppermute | solution.py:117
  99.4 1.4 collective-permute-start.28
  100.1 1.6 collective-permute-start.9
  100.8 1.1 collective-permute-start.29
  101.7 19.0 %slice-start.1 = ((s8[6291456]{0:T(1024)(128)(4,1)}), s8[2097152]{0:T(1024)(128)(4,1)S(1)}, s32[]{:S(2)}) async-start(s8[6291456]{0:T(1024)(128)(4,1)} %bitcast.153), calls=%async_computation.1 | async-start | bytes 4194304
  102.1 17.9 %collective-permute-start.30 = (bf16[4,64,3072]{2,1,0:T(8,128)(2,1)S(1)}, bf16[4,64,3072]{2,1,0:T(8,128)(2,1)S(1)}, u32[]{:S(2)}, u32[]{:S(2)}) collective-permute-start(bf16[4,64,3072]{2,1,0:T(8,128)(2,1)S(1)} %fusion.7), channel_id=1, source_target_pairs={{0,4},{4,0},{1,5},{5,1},{2,6},{6,2},{3,7},{7,3},{8,12},{12,8},{9,1... | collective-permute-start | bytes 4718600 | tf_op jit(solution)/shard_map/ppermute | solution.py:109
  117.0 7.0 %collective-permute-start.10 = (bf16[4,64,3072]{2,1,0:T(8,128)(2,1)S(1)}, bf16[4,64,3072]{2,1,0:T(8,128)(2,1)S(1)}, u32[]{:S(2)}, u32[]{:S(2)}) collective-permute-start(bf16[4,64,3072]{2,1,0:T(8,128)(2,1)S(1)} %fusion.13), channel_id=1, source_target_pairs={{0,4},{4,0},{1,5},{5,1},{2,6},{6,2},{3,7},{7,3},{8,12},{12,8},{9,1... | collective-permute-start | bytes 4718600 | tf_op jit(solution)/shard_map/ppermute | solution.py:109
  122.5 9.2 %collective-permute-start.31 = (bf16[256,1024]{1,0:T(8,128)(2,1)S(1)}, bf16[256,1024]{1,0:T(8,128)(2,1)S(1)}, u32[]{:S(2)}, u32[]{:S(2)}) collective-permute-start(bf16[256,1024]{1,0:T(8,128)(2,1)S(1)} %convolution_convert_fusion), channel_id=1, source_target_pairs={{0,1},{1,0},{2,3},{3,2},{4,6},{5,7},{6,4},{7,5},{8,9},{9,8},{10,11... | collective-permute-start | bytes 1572872 | tf_op jit(solution)/shard_map/ppermute | solution.py:168
  126.4 14.1 %collective-permute-start.11 = (bf16[256,1024]{1,0:T(8,128)(2,1)S(1)}, bf16[256,1024]{1,0:T(8,128)(2,1)S(1)}, u32[]{:S(2)}, u32[]{:S(2)}) collective-permute-start(bf16[256,1024]{1,0:T(8,128)(2,1)S(1)} %convolution_convert_fusion.1), channel_id=1, source_target_pairs={{0,1},{1,0},{2,3},{3,2},{4,6},{5,7},{6,4},{7,5},{8,9},{9,8},{10,11... | collective-permute-start | bytes 1572872 | tf_op jit(solution)/shard_map/ppermute | solution.py:168
  131.9 18.5 %collective-permute-start.32 = (bf16[256,1024]{1,0:T(8,128)(2,1)S(1)}, bf16[256,1024]{1,0:T(8,128)(2,1)S(1)}, u32[]{:S(2)}, u32[]{:S(2)}) collective-permute-start(bf16[256,1024]{1,0:T(8,128)(2,1)S(1)} %add_convert_fusion), channel_id=1, source_target_pairs={{0,2},{1,3},{2,0},{3,1},{4,5},{5,4},{6,7},{7,6},{8,10},{9,11},{10,... | collective-permute-start | bytes 1572872 | tf_op jit(solution)/shard_map/ppermute | solution.py:168
  140.8 9.3 %copy-start.7 = (f32[1024]{0:T(1024)S(1)}, f32[1024]{0:T(1024)}, u32[]{:S(2)}) copy-start(f32[1024]{0:T(1024)} %param.13) | copy-start | bytes 12292
  140.8 9.2 %collective-permute-start.12 = (bf16[256,1024]{1,0:T(8,128)(2,1)S(1)}, bf16[256,1024]{1,0:T(8,128)(2,1)S(1)}, u32[]{:S(2)}, u32[]{:S(2)}) collective-permute-start(bf16[256,1024]{1,0:T(8,128)(2,1)S(1)} %add_convert_fusion.1), channel_id=1, source_target_pairs={{0,2},{1,3},{2,0},{3,1},{4,5},{5,4},{6,7},{7,6},{8,10},{9,11},{10,... | collective-permute-start | bytes 1572872 | tf_op jit(solution)/shard_map/ppermute | solution.py:168
  152.2 3.5 %collective-permute-start.13 = (bf16[4,64,3072]{2,1,0:T(8,128)(2,1)S(1)}, bf16[4,64,3072]{2,1,0:T(8,128)(2,1)S(1)}, u32[]{:S(2)}, u32[]{:S(2)}) collective-permute-start(bf16[4,64,3072]{2,1,0:T(8,128)(2,1)S(1)} %bitcast.186), channel_id=1, source_target_pairs={{0,4},{4,0},{1,5},{5,1},{2,6},{6,2},{3,7},{7,3},{8,12},{12,8},{9,1... | collective-permute-start | bytes 4718600 | tf_op jit(solution)/shard_map/ppermute | solution.py:109
  154.9 3.6 %collective-permute-start.33 = (bf16[4,64,3072]{2,1,0:T(8,128)(2,1)S(1)}, bf16[4,64,3072]{2,1,0:T(8,128)(2,1)S(1)}, u32[]{:S(2)}, u32[]{:S(2)}) collective-permute-start(bf16[4,64,3072]{2,1,0:T(8,128)(2,1)S(1)} %bitcast.185), channel_id=1, source_target_pairs={{0,4},{4,0},{1,5},{5,1},{2,6},{6,2},{3,7},{7,3},{8,12},{12,8},{9,1... | collective-permute-start | bytes 4718600 | tf_op jit(solution)/shard_map/ppermute | solution.py:109
  155.8 7.0 %collective-permute-start.14 = (bf16[64,3072]{1,0:T(8,128)(2,1)S(1)}, bf16[64,3072]{1,0:T(8,128)(2,1)S(1)}, u32[]{:S(2)}, u32[]{:S(2)}) collective-permute-start(bf16[64,3072]{1,0:T(8,128)(2,1)S(1)} %fusion.38), channel_id=1, source_target_pairs={{0,8},{28,20},{1,9},{29,21},{2,10},{30,22},{3,11},{31,23}} | collective-permute-start | bytes 1179656 | tf_op jit(solution)/shard_map/ppermute | solution.py:117
  158.6 9.0 %collective-permute-start.34 = (bf16[64,3072]{1,0:T(8,128)(2,1)S(1)}, bf16[64,3072]{1,0:T(8,128)(2,1)S(1)}, u32[]{:S(2)}, u32[]{:S(2)}) collective-permute-start(bf16[64,3072]{1,0:T(8,128)(2,1)S(1)} %fusion.30), channel_id=1, source_target_pairs={{0,8},{28,20},{1,9},{29,21},{2,10},{30,22},{3,11},{31,23}} | collective-permute-start | bytes 1179656 | tf_op jit(solution)/shard_map/ppermute | solution.py:117
  162.8 57.4 %slice-start.4 = ((s8[6291456]{0:T(1024)(128)(4,1)}), s8[4194304]{0:T(1024)(128)(4,1)S(1)}, s32[]{:S(2)}) async-start(s8[6291456]{0:T(1024)(128)(4,1)} %bitcast.157), calls=%async_computation.4 | async-start | bytes 8388608
  162.9 9.9 %collective-permute-start.15 = (bf16[64,3072]{1,0:T(8,128)(2,1)S(1)}, bf16[64,3072]{1,0:T(8,128)(2,1)S(1)}, u32[]{:S(2)}, u32[]{:S(2)}) collective-permute-start(bf16[64,3072]{1,0:T(8,128)(2,1)S(1)} %fusion.40), channel_id=1, source_target_pairs={{0,8},{28,20},{8,16},{20,12},{1,9},{29,21},{9,17},{21,13},{2,10},{... | collective-permute-start | bytes 1179656 | tf_op jit(solution)/shard_map/ppermute | solution.py:117
  167.8 9.9 %collective-permute-start.35 = (bf16[64,3072]{1,0:T(8,128)(2,1)S(1)}, bf16[64,3072]{1,0:T(8,128)(2,1)S(1)}, u32[]{:S(2)}, u32[]{:S(2)}) collective-permute-start(bf16[64,3072]{1,0:T(8,128)(2,1)S(1)} %fusion.32), channel_id=1, source_target_pairs={{0,8},{28,20},{8,16},{20,12},{1,9},{29,21},{9,17},{21,13},{2,10},{... | collective-permute-start | bytes 1179656 | tf_op jit(solution)/shard_map/ppermute | solution.py:117
  172.9 47.3 %slice-start.2 = ((s8[6291456]{0:T(1024)(128)(4,1)}), s8[4194304]{0:T(1024)(128)(4,1)S(1)}, s32[]{:S(2)}) async-start(s8[6291456]{0:T(1024)(128)(4,1)} %bitcast.155), calls=%async_computation.2 | async-start | bytes 8388608
  173.0 9.9 %collective-permute-start.16 = (bf16[64,3072]{1,0:T(8,128)(2,1)S(1)}, bf16[64,3072]{1,0:T(8,128)(2,1)S(1)}, u32[]{:S(2)}, u32[]{:S(2)}) collective-permute-start(bf16[64,3072]{1,0:T(8,128)(2,1)S(1)} %fusion.42), channel_id=1, source_target_pairs={{0,8},{28,20},{8,16},{20,12},{16,24},{12,4},{1,9},{29,21},{9,17},{... | collective-permute-start | bytes 1179656 | tf_op jit(solution)/shard_map/ppermute | solution.py:117
  177.9 9.3 %collective-permute-start.36 = (bf16[64,3072]{1,0:T(8,128)(2,1)S(1)}, bf16[64,3072]{1,0:T(8,128)(2,1)S(1)}, u32[]{:S(2)}, u32[]{:S(2)}) collective-permute-start(bf16[64,3072]{1,0:T(8,128)(2,1)S(1)} %fusion.34), channel_id=1, source_target_pairs={{0,8},{28,20},{8,16},{20,12},{16,24},{12,4},{1,9},{29,21},{9,17},{... | collective-permute-start | bytes 1179656 | tf_op jit(solution)/shard_map/ppermute | solution.py:117
  183.0 4.2 %collective-permute-start.17 = (bf16[64,3072]{1,0:T(8,128)(2,1)S(1)}, bf16[64,3072]{1,0:T(8,128)(2,1)S(1)}, u32[]{:S(2)}, u32[]{:S(2)}) collective-permute-start(bf16[64,3072]{1,0:T(8,128)(2,1)S(1)} %collective-permute-done.16), channel_id=1, source_target_pairs={{0,4},{4,0},{1,5},{5,1},{2,6},{6,2},{3,7},{7,3},{8,12},{12,8},{9,1... | collective-permute-start | bytes 1179656 | tf_op jit(solution)/shard_map/ppermute | solution.py:109
  187.2 4.7 %collective-permute-start.37 = (bf16[64,3072]{1,0:T(8,128)(2,1)S(1)}, bf16[64,3072]{1,0:T(8,128)(2,1)S(1)}, u32[]{:S(2)}, u32[]{:S(2)}) collective-permute-start(bf16[64,3072]{1,0:T(8,128)(2,1)S(1)} %collective-permute-done.36), channel_id=1, source_target_pairs={{0,4},{4,0},{1,5},{5,1},{2,6},{6,2},{3,7},{7,3},{8,12},{12,8},{9,1... | collective-permute-start | bytes 1179656 | tf_op jit(solution)/shard_map/ppermute | solution.py:109
  187.4 9.7 %collective-permute-start.18 = (bf16[64,3072]{1,0:T(8,128)(2,1)S(1)}, bf16[64,3072]{1,0:T(8,128)(2,1)S(1)}, u32[]{:S(2)}, u32[]{:S(2)}) collective-permute-start(bf16[64,3072]{1,0:T(8,128)(2,1)S(1)} %fusion.45), channel_id=1, source_target_pairs={{0,8},{28,20},{8,16},{20,12},{16,24},{12,4},{1,9},{29,21},{9,17},{... | collective-permute-start | bytes 1179656 | tf_op jit(solution)/shard_map/ppermute | solution.py:117
  191.9 28.3 %slice-start.3 = ((s8[6291456]{0:T(1024)(128)(4,1)}), s8[2097152]{0:T(1024)(128)(4,1)S(1)}, s32[]{:S(2)}) async-start(s8[6291456]{0:T(1024)(128)(4,1)} %bitcast.155), calls=%async_computation.3 | async-start | bytes 4194304
  191.9 28.3 %slice-start.5 = ((s8[6291456]{0:T(1024)(128)(4,1)}), s8[2097152]{0:T(1024)(128)(4,1)S(1)}, s32[]{:S(2)}) async-start(s8[6291456]{0:T(1024)(128)(4,1)} %bitcast.157), calls=%async_computation.5 | async-start | bytes 4194304
  192.2 9.2 %collective-permute-start.38 = (bf16[64,3072]{1,0:T(8,128)(2,1)S(1)}, bf16[64,3072]{1,0:T(8,128)(2,1)S(1)}, u32[]{:S(2)}, u32[]{:S(2)}) collective-permute-start(bf16[64,3072]{1,0:T(8,128)(2,1)S(1)} %fusion.37), channel_id=1, source_target_pairs={{0,8},{28,20},{8,16},{20,12},{16,24},{12,4},{1,9},{29,21},{9,17},{... | collective-permute-start | bytes 1179656 | tf_op jit(solution)/shard_map/ppermute | solution.py:117
  197.1 4.9 %collective-permute-start.19 = (bf16[64,3072]{1,0:T(8,128)(2,1)S(1)}, bf16[64,3072]{1,0:T(8,128)(2,1)S(1)}, u32[]{:S(2)}, u32[]{:S(2)}) collective-permute-start(bf16[64,3072]{1,0:T(8,128)(2,1)S(1)} %collective-permute-done.18), channel_id=1, source_target_pairs={{8,16},{20,12},{16,24},{12,4},{9,17},{21,13},{17,25},{13,5},{10,18... | collective-permute-start | bytes 1179656 | tf_op jit(solution)/shard_map/ppermute | solution.py:117
  201.3 1.4 collective-permute-start.39
  202.0 1.4 collective-permute-start.20
  202.7 0.9 collective-permute-start.40
  203.8 36.4 %collective-permute-start.41 = (bf16[4,64,3072]{2,1,0:T(8,128)(2,1)S(1)}, bf16[4,64,3072]{2,1,0:T(8,128)(2,1)S(1)}, u32[]{:S(2)}, u32[]{:S(2)}) collective-permute-start(bf16[4,64,3072]{2,1,0:T(8,128)(2,1)S(1)} %fusion.4), channel_id=1, source_target_pairs={{0,4},{4,0},{1,5},{5,1},{2,6},{6,2},{3,7},{7,3},{8,12},{12,8},{9,1... | collective-permute-start | bytes 4718600 | tf_op jit(solution)/shard_map/ppermute | solution.py:109
  219.0 21.9 %collective-permute-start.21 = (bf16[4,64,3072]{2,1,0:T(8,128)(2,1)S(1)}, bf16[4,64,3072]{2,1,0:T(8,128)(2,1)S(1)}, u32[]{:S(2)}, u32[]{:S(2)}) collective-permute-start(bf16[4,64,3072]{2,1,0:T(8,128)(2,1)S(1)} %fusion.10), channel_id=1, source_target_pairs={{0,4},{4,0},{1,5},{5,1},{2,6},{6,2},{3,7},{7,3},{8,12},{12,8},{9,1... | collective-permute-start | bytes 4718600 | tf_op jit(solution)/shard_map/ppermute | solution.py:109
  236.9 5.2 %slice-start.8 = ((s8[6291456]{0:T(1024)(128)(4,1)}), s8[4194304]{0:T(1024)(128)(4,1)S(1)}, s32[]{:S(2)}) async-start(s8[6291456]{0:T(1024)(128)(4,1)} %bitcast.179), calls=%async_computation.8 | async-start | bytes 8388608
  236.9 5.2 %slice-start.9 = ((s8[6291456]{0:T(1024)(128)(4,1)}), s8[2097152]{0:T(1024)(128)(4,1)S(1)}, s32[]{:S(2)}) async-start(s8[6291456]{0:T(1024)(128)(4,1)} %bitcast.179), calls=%async_computation.9 | async-start | bytes 4194304
  242.1 2.8 %copy-start.2 = (bf16[1024,3072]{1,0:T(8,128)(2,1)S(1)}, bf16[1024,3072]{1,0:T(8,128)(2,1)}, u32[]{:S(2)}) copy-start(bf16[1024,3072]{1,0:T(8,128)(2,1)} %refs_5_.7) | copy-start | bytes 18874372
  244.9 15.2 %copy-start.1 = (bf16[256,1024]{1,0:T(8,128)(2,1)S(1)}, bf16[256,1024]{1,0:T(8,128)(2,1)}, u32[]{:S(2)}) copy-start(bf16[256,1024]{1,0:T(8,128)(2,1)} %param.9) | copy-start | bytes 1572868
